TPU v7x, 128 devices: a whole 4x4x4 slice. The times are simulated.
128 devices in a mesh: slab: 32 (over y, x, core), probe: 4 (over z).
Axes of the slice: x: 4, y: 4, z: 4, core: 2. Of those that a mesh axis runs over, the one named last changes fastest.
Arguments:
- probe_fields: bfloat16 [256, 128, 8192], P('probe', 'slab'), may hold values from -6 to 6
- sensor_rows: int32 [4096], replicated, may hold values from 0 to 126, as said below
- sensor_cols: int32 [4096], replicated, may hold values from 0 to 8190
- row_frac: float32 [4096], replicated, may hold values from 0 to 1
- col_frac: float32 [4096], replicated, may hold values from 0 to 1
- sensor_weights: float32 [4096], replicated, may hold values from 0.05 to 1
- owner_order: int32 [4096], replicated, may hold values from 0 to 4095, as said below
Outputs:
- adjoint_sources: bfloat16 [256, 128, 8192], P('probe', 'slab')
- observed: float32 [256, 4096], P('probe', 'slab')
- trace_mean: float32 [], replicated
Inputs may be any that keep to these rules, and one draw needn't show every extreme that they name: `sensor_rows`: rows run from 0 to 126. The sensors whose row lies in one slab of 4 rows number at most 512, and some slab holds exactly 512. `owner_order`: A permutation. The 4096 // 32 slots of one owner name at most 16 sensors whose row lies in any one slab, and every owner reaches 16 for some slab.
All inputs are finite; a program needn't handle non-finite values.
Results may differ from a plain program's by a relative error of at most 0.0068.
Values sent between devices are 32-bit elements; how exact they have to be, the bound alone decides.
A program may use at most 64 MiB of HBM per device.

v0:
```python
import jax
import jax.numpy as jnp
from jax import lax
from jax.sharding import Mesh
from jax.sharding import PartitionSpec as P

SLAB = ("slab_0", "slab_1", "slab_2")
SLAB_PROBE = ("slab_0", "slab_1", "slab_2", "probe")


def in_blocks(x, dim, length):
    before, after = (x.shape[:dim], x.shape[dim + 1 :])
    return jnp.moveaxis(x.reshape(*before, length, -1, *after), dim, 0)


def summed_on_arrival(x, axis, dim):
    pieces = in_blocks(x, dim, lax.axis_size(axis))
    arrived = lax.all_to_all(pieces, axis, split_axis=0, concat_axis=0, tiled=True)
    return arrived.sum(axis=0)


def by_axis(x, axes):
    for axis in axes:
        x = lax.psum(x, axis)
    return x


def in_order(pieces, dim):
    lengths = list(pieces.shape[1:])
    lengths[dim] *= pieces.shape[0]
    return jnp.moveaxis(pieces, 0, dim).reshape(lengths)


def from_everyone(x, axis):
    length = lax.axis_size(axis)
    return lax.all_to_all(jnp.broadcast_to(x[None], (length, *x.shape)), axis, 0, 0, tiled=True)


def gather_directly(x, axis, dim):
    return in_order(from_everyone(x, axis), dim)


def column_table(columns, fractions, start, count, across):
    low_value = (1.0 - fractions).astype(jnp.bfloat16)
    high_value = fractions.astype(jnp.bfloat16)
    zero_value = jnp.zeros((), jnp.bfloat16)
    if across:
        cells = start + lax.broadcasted_iota(jnp.int32, (columns.shape[0], count), 1)
        where_col = columns[:, None]
        low_b = low_value[:, None]
        high_b = high_value[:, None]
    else:
        cells = start + lax.broadcasted_iota(jnp.int32, (count, columns.shape[0]), 0)
        where_col = columns[None, :]
        low_b = low_value[None, :]
        high_b = high_value[None, :]
    return jnp.where(
        cells == where_col, low_b, jnp.where(cells == where_col + 1, high_b, zero_value)
    )


def adjoint_grid(sources, columns, fractions, width):
    column_block = min(1024, width)

    def adjoint_block(number, result):
        begin = number * column_block
        table = column_table(columns, fractions, begin, column_block, True)
        piece = jnp.dot(sources, table, preferred_element_type=jnp.float32)
        return lax.dynamic_update_slice_in_dim(result, piece.astype(jnp.bfloat16), begin, 1)

    return lax.fori_loop(
        0, width // column_block, adjoint_block, jnp.zeros((sources.shape[0], width), jnp.bfloat16)
    )


def body(probe_fields, sensor_rows, sensor_cols, row_frac, col_frac, sensor_weights, owner_order):
    probe_count, row_count, width = probe_fields.shape
    sensor_count = sensor_rows.shape[0]
    depth = probe_count * row_count
    owned_rows = sensor_rows[owner_order]
    owned_cols = sensor_cols[owner_order]
    owned_rowfrac = row_frac[owner_order]
    owned_colfrac = col_frac[owner_order]
    owned_weights = sensor_weights[owner_order]
    slab_index = lax.axis_index(SLAB)
    first_row = slab_index * row_count
    slab_count = lax.axis_size(SLAB)
    own_count = sensor_count // slab_count
    own_begin = slab_index * own_count
    total_count = probe_count * lax.axis_size("probe") * sensor_count
    local_rows = first_row + lax.broadcasted_iota(jnp.int32, (row_count, sensor_count), 0)
    row_weights = jnp.where(local_rows == owned_rows[None, :], 1.0 - owned_rowfrac[None, :], 0.0)
    row_weights = row_weights + jnp.where(
        local_rows == owned_rows[None, :] + 1, owned_rowfrac[None, :], 0.0
    )
    flat_fields = probe_fields.reshape(depth, width)
    sensor_block = min(512, sensor_count)

    def forward_block(number, partial_value):
        begin = number * sensor_block
        cols_block = lax.dynamic_slice_in_dim(owned_cols, begin, sensor_block)
        frac_block = lax.dynamic_slice_in_dim(owned_colfrac, begin, sensor_block)
        table = column_table(cols_block, frac_block, 0, width, False)
        along = jnp.dot(flat_fields, table, preferred_element_type=jnp.float32)
        along = along.reshape(probe_count, row_count, sensor_block)
        weights_block = lax.dynamic_slice_in_dim(row_weights, begin, sensor_block, 1)
        summed = jnp.sum(along * weights_block[None, :, :], axis=1)
        return lax.dynamic_update_slice_in_dim(partial_value, summed, begin, 1)

    partial_value = lax.fori_loop(
        0,
        sensor_count // sensor_block,
        forward_block,
        jnp.zeros((probe_count, sensor_count), jnp.float32),
    )
    observed = summed_on_arrival(partial_value, SLAB, 1)
    own_weights = lax.dynamic_slice_in_dim(owned_weights, own_begin, own_count)
    spread_own = observed * own_weights[None, :]
    total = by_axis(jnp.sum(spread_own * observed), SLAB_PROBE)
    spread = gather_directly(spread_own, SLAB, 1)
    sources = (spread[:, None, :] * row_weights[None, :, :]).astype(jnp.bfloat16)
    sources = sources.reshape(depth, sensor_count)
    result = adjoint_grid(sources, owned_cols, owned_colfrac, width)
    trace_mean = total / total_count
    adjoint_sources = result.reshape(probe_count, row_count, width)
    return (adjoint_sources, observed, trace_mean)


def solution(mesh):
    torus = Mesh(
        mesh.devices.reshape(4, 4, 2, mesh.shape["probe"]), ("slab_0", "slab_1", "slab_2", "probe")
    )
    placed = (P("probe", SLAB, None), P(), P(), P(), P(), P(), P())
    return jax.shard_map(
        body,
        mesh=torus,
        in_specs=placed,
        out_specs=(P("probe", SLAB, None), P("probe", SLAB), P()),
        check_vma=False,
    )
```

profile of v0, /device:TPU:1, one launch (start us, length us, event | category | flops | bytes accessed | tf_op | source)
XLA Modules:
  0.0 336.7 jit_solution(1207151873596464338)
XLA Ops:
  1.4 23.0 %gather_fusion.1 = f32[4096]{0:T(1024)S(1)} fusion(f32[4096]{0:T(1024)S(1)} %copy-done, s32[4096]{0:T(1024)S(1)} %fusion.23), kind=kCustom, calls=%fused_computation.1 | custom fusion | bytes 49152 | tf_op jit(solution)/shard_map/gather | solution.py:83
  24.5 23.0 %gather_fusion.3 = f32[4096]{0:T(1024)S(1)} fusion(f32[4096]{0:T(1024)S(1)} %copy-done.1, s32[4096]{0:T(1024)S(1)} %fusion.23), kind=kCustom, calls=%fused_computation.3 | custom fusion | bytes 49152 | tf_op jit(solution)/shard_map/gather | solution.py:82
  47.5 23.0 %gather_fusion.2 = s32[4096]{0:T(1024)S(1)} fusion(s32[4096]{0:T(1024)S(1)} %copy-done.2, s32[4096]{0:T(1024)S(1)} %fusion.23), kind=kCustom, calls=%fused_computation.2 | custom fusion | bytes 49152 | tf_op jit(solution)/shard_map/gather | solution.py:80
  70.6 23.0 %gather_fusion = s32[4096]{0:T(1024)S(1)} fusion(s32[4096]{0:T(1024)S(1)} %copy-done.3, s32[4096]{0:T(1024)S(1)} %fusion.23), kind=kCustom, calls=%fused_computation | custom fusion | bytes 49152 | tf_op jit(solution)/shard_map/gather | solution.py:81
  93.6 6.9 %reshape.166 = bf16[256,8192]{1,0:T(8,128)(2,1)} reshape(bf16[64,4,8192]{2,1,0:T(4,128)(2,1)} %param.11) | data formatting | bytes 8388608 | tf_op jit(solution)/shard_map/reshape | solution.py:96
  100.7 48.5 %while.28 = (s32[]{:T(128)}, f32[64,4096]{1,0:T(8,128)S(1)}, s32[4096]{0:T(1024)S(1)}, f32[4096]{0:T(1024)S(1)}, bf16[256,8192]{1,0:T(8,128)(2,1)}, /*index=5*/f...) while((s32[]{:T(128)}, f32[64,4096]{1,0:T(8,128)S(1)}, s32[4096]{0:T(1024)S(1)}, ...), condition=%wide.region_2.3_spmd, body=%wide.region_0.2_spmd.sunk | while | flops 2164491776 | bytes 6726823 | solution.py:110
  100.9 5.3 %fusion.34 = f32[256,512]{1,0:T(8,128)S(1)} fusion(bf16[256,8192]{1,0:T(8,128)(2,1)} %get-tuple-element.389, s32[512]{0:T(512)S(1)} %get-tuple-element.356, s32[512]{0:T(512)S(1)} %get-tuple-element.357, bf16[512]{0:T(512)(128)(2,1)S(1)} %dynamic_slice.37, bf16[512]{0:T(512)(128)(2,1)S(1)} %subtract_convert_fusion.4), kind=kOutput, calls=%fused_computation.14.clone.1 | convolution fusion | flops 2164260864 | bytes 4724736 | tf_op jit(solution)/shard_map/while/body/eval_jaxpr/dot_general | solution.py:104
  107.0 5.3 %fusion.34 = f32[256,512]{1,0:T(8,128)S(1)} fusion(bf16[256,8192]{1,0:T(8,128)(2,1)} %get-tuple-element.389, s32[512]{0:T(512)S(1)} %get-tuple-element.356, s32[512]{0:T(512)S(1)} %get-tuple-element.357, bf16[512]{0:T(512)(128)(2,1)S(1)} %dynamic_slice.37, bf16[512]{0:T(512)(128)(2,1)S(1)} %subtract_convert_fusion.4), kind=kOutput, calls=%fused_computation.14.clone.1 | convolution fusion | flops 2164260864 | bytes 4724736 | tf_op jit(solution)/shard_map/while/body/eval_jaxpr/dot_general | solution.py:104
  113.1 5.3 %fusion.34 = f32[256,512]{1,0:T(8,128)S(1)} fusion(bf16[256,8192]{1,0:T(8,128)(2,1)} %get-tuple-element.389, s32[512]{0:T(512)S(1)} %get-tuple-element.356, s32[512]{0:T(512)S(1)} %get-tuple-element.357, bf16[512]{0:T(512)(128)(2,1)S(1)} %dynamic_slice.37, bf16[512]{0:T(512)(128)(2,1)S(1)} %subtract_convert_fusion.4), kind=kOutput, calls=%fused_computation.14.clone.1 | convolution fusion | flops 2164260864 | bytes 4724736 | tf_op jit(solution)/shard_map/while/body/eval_jaxpr/dot_general | solution.py:104
  119.1 5.3 %fusion.34 = f32[256,512]{1,0:T(8,128)S(1)} fusion(bf16[256,8192]{1,0:T(8,128)(2,1)} %get-tuple-element.389, s32[512]{0:T(512)S(1)} %get-tuple-element.356, s32[512]{0:T(512)S(1)} %get-tuple-element.357, bf16[512]{0:T(512)(128)(2,1)S(1)} %dynamic_slice.37, bf16[512]{0:T(512)(128)(2,1)S(1)} %subtract_convert_fusion.4), kind=kOutput, calls=%fused_computation.14.clone.1 | convolution fusion | flops 2164260864 | bytes 4724736 | tf_op jit(solution)/shard_map/while/body/eval_jaxpr/dot_general | solution.py:104
  125.2 5.3 %fusion.34 = f32[256,512]{1,0:T(8,128)S(1)} fusion(bf16[256,8192]{1,0:T(8,128)(2,1)} %get-tuple-element.389, s32[512]{0:T(512)S(1)} %get-tuple-element.356, s32[512]{0:T(512)S(1)} %get-tuple-element.357, bf16[512]{0:T(512)(128)(2,1)S(1)} %dynamic_slice.37, bf16[512]{0:T(512)(128)(2,1)S(1)} %subtract_convert_fusion.4), kind=kOutput, calls=%fused_computation.14.clone.1 | convolution fusion | flops 2164260864 | bytes 4724736 | tf_op jit(solution)/shard_map/while/body/eval_jaxpr/dot_general | solution.py:104
  131.3 5.3 %fusion.34 = f32[256,512]{1,0:T(8,128)S(1)} fusion(bf16[256,8192]{1,0:T(8,128)(2,1)} %get-tuple-element.389, s32[512]{0:T(512)S(1)} %get-tuple-element.356, s32[512]{0:T(512)S(1)} %get-tuple-element.357, bf16[512]{0:T(512)(128)(2,1)S(1)} %dynamic_slice.37, bf16[512]{0:T(512)(128)(2,1)S(1)} %subtract_convert_fusion.4), kind=kOutput, calls=%fused_computation.14.clone.1 | convolution fusion | flops 2164260864 | bytes 4724736 | tf_op jit(solution)/shard_map/while/body/eval_jaxpr/dot_general | solution.py:104
  137.4 5.3 %fusion.34 = f32[256,512]{1,0:T(8,128)S(1)} fusion(bf16[256,8192]{1,0:T(8,128)(2,1)} %get-tuple-element.389, s32[512]{0:T(512)S(1)} %get-tuple-element.356, s32[512]{0:T(512)S(1)} %get-tuple-element.357, bf16[512]{0:T(512)(128)(2,1)S(1)} %dynamic_slice.37, bf16[512]{0:T(512)(128)(2,1)S(1)} %subtract_convert_fusion.4), kind=kOutput, calls=%fused_computation.14.clone.1 | convolution fusion | flops 2164260864 | bytes 4724736 | tf_op jit(solution)/shard_map/while/body/eval_jaxpr/dot_general | solution.py:104
  143.4 5.3 %fusion.34 = f32[256,512]{1,0:T(8,128)S(1)} fusion(bf16[256,8192]{1,0:T(8,128)(2,1)} %get-tuple-element.389, s32[512]{0:T(512)S(1)} %get-tuple-element.356, s32[512]{0:T(512)S(1)} %get-tuple-element.357, bf16[512]{0:T(512)(128)(2,1)S(1)} %dynamic_slice.37, bf16[512]{0:T(512)(128)(2,1)S(1)} %subtract_convert_fusion.4), kind=kOutput, calls=%fused_computation.14.clone.1 | convolution fusion | flops 2164260864 | bytes 4724736 | tf_op jit(solution)/shard_map/while/body/eval_jaxpr/dot_general | solution.py:104
  151.0 8.6 %all-to-all-start = ((f32[32,64,128]{2,1,0:T(8,128)}), f32[32,64,128]{2,1,0:T(8,128)S(1)}, u32[]{:S(2)}, u32[]{:S(2)}) async-start(f32[32,64,128]{2,1,0:T(8,128)} %copy.13), calls=%async_computation | async-start | bytes 2097152 | tf_op jit(solution)/shard_map/all_to_all | solution.py:18
  159.6 23.0 %gather_fusion.4 = f32[4096]{0:T(1024)S(1)} fusion(f32[4096]{0:T(1024)S(1)} %copy-done.4, s32[4096]{0:T(1024)S(1)} %fusion.23), kind=kCustom, calls=%fused_computation.4 | custom fusion | bytes 49152 | tf_op jit(solution)/shard_map/gather | solution.py:84
  184.5 7.4 %all-to-all-start.1 = ((f32[32,64,128]{2,1,0:T(8,128)}), f32[32,64,128]{2,1,0:T(8,128)S(1)}, u32[]{:S(2)}, u32[]{:S(2)}) async-start(f32[32,64,128]{2,1,0:T(8,128)} %broadcast_in_dim.161), calls=%async_computation.1 | async-start | bytes 2097152 | tf_op jit(solution)/shard_map/all_to_all | solution.py:36
  191.9 11.8 %psum.28 = f32[]{:T(128)} all-reduce(f32[]{:T(128)} %get-tuple-element.279), channel_id=1, replica_groups=mesh['slab_0'=4,'slab_1'=4,'slab_2'=2,'probe'=4] {'slab_0'}, use_global_device_ids=true, to_apply=%region_7.8 | all-reduce | flops 1 | bytes 8 | tf_op jit(solution)/shard_map/psum | solution.py:24
  203.7 12.4 %psum.29 = f32[]{:T(128)} all-reduce(f32[]{:T(128)} %psum.28), channel_id=1, replica_groups=mesh['slab_0'=4,'slab_1'=4,'slab_2'=2,'probe'=4] {'slab_1'}, use_global_device_ids=true, to_apply=%region_8.9 | all-reduce | flops 1 | bytes 8 | tf_op jit(solution)/shard_map/psum | solution.py:24
  216.1 7.5 %psum.30 = f32[]{:T(128)} all-reduce(f32[]{:T(128)} %psum.29), channel_id=1, replica_groups=mesh['slab_0'=4,'slab_1'=4,'slab_2'=2,'probe'=4] {'slab_2'}, use_global_device_ids=true, to_apply=%region_9.10 | all-reduce | flops 1 | bytes 8 | tf_op jit(solution)/shard_map/psum | solution.py:24
  223.7 10.6 %psum.31 = f32[]{:T(128)} all-reduce(f32[]{:T(128)} %psum.30), channel_id=1, replica_groups=mesh['slab_0'=4,'slab_1'=4,'slab_2'=2,'probe'=4] {'probe'}, use_global_device_ids=true, to_apply=%region_10.11 | all-reduce | flops 1 | bytes 8 | tf_op jit(solution)/shard_map/psum | solution.py:24
  235.0 2.4 broadcast_in_dim.155.clone
  237.4 91.1 %while.29 = (s32[]{:T(128)}, bf16[256,8192]{1,0:T(8,128)(2,1)}, s32[4096]{0:T(1024)S(1)}, f32[4096]{0:T(1024)S(1)}, bf16[4096,1]{0,1:T(2,128)(2,1)S(1)}, /*index...) while((s32[]{:T(128)}, bf16[256,8192]{1,0:T(8,128)(2,1)}, ...), condition=%wide.region_5.6_spmd.clone, body=%wide.region_4.5_spmd.clone.sunk | while | flops 2166633472 | bytes 12255405 | solution.py:71
  240.6 7.0 %fusion.36 = bf16[256,1024]{0,1:T(8,128)(2,1)S(1)} fusion(bf16[256,4096]{1,0:T(8,128)(2,1)} %convert_element_type.94, s32[1024]{0:T(1024)S(1)} %iota_add_fusion.3, s32[4096]{0:T(1024)S(1)} %broadcast_add_fusion.6, s32[4096]{0:T(1024)S(1)} %get-tuple-element.421, bf16[4096]{0:T(1024)(128)(2,1)S(1)} %reduce.2, ...), kind=kOutput, calls=%fused_computation.33.clone.1 | convolution fusion | flops 2164523008 | bytes 2674688 | tf_op jit(solution)/shard_map/while/body/eval_jaxpr/dot_general | solution.py:68
  252.1 7.0 %fusion.36 = bf16[256,1024]{0,1:T(8,128)(2,1)S(1)} fusion(bf16[256,4096]{1,0:T(8,128)(2,1)} %convert_element_type.94, s32[1024]{0:T(1024)S(1)} %iota_add_fusion.3, s32[4096]{0:T(1024)S(1)} %broadcast_add_fusion.6, s32[4096]{0:T(1024)S(1)} %get-tuple-element.421, bf16[4096]{0:T(1024)(128)(2,1)S(1)} %reduce.2, ...), kind=kOutput, calls=%fused_computation.33.clone.1 | convolution fusion | flops 2164523008 | bytes 2674688 | tf_op jit(solution)/shard_map/while/body/eval_jaxpr/dot_general | solution.py:68
  263.4 7.0 %fusion.36 = bf16[256,1024]{0,1:T(8,128)(2,1)S(1)} fusion(bf16[256,4096]{1,0:T(8,128)(2,1)} %convert_element_type.94, s32[1024]{0:T(1024)S(1)} %iota_add_fusion.3, s32[4096]{0:T(1024)S(1)} %broadcast_add_fusion.6, s32[4096]{0:T(1024)S(1)} %get-tuple-element.421, bf16[4096]{0:T(1024)(128)(2,1)S(1)} %reduce.2, ...), kind=kOutput, calls=%fused_computation.33.clone.1 | convolution fusion | flops 2164523008 | bytes 2674688 | tf_op jit(solution)/shard_map/while/body/eval_jaxpr/dot_general | solution.py:68
  274.8 7.0 %fusion.36 = bf16[256,1024]{0,1:T(8,128)(2,1)S(1)} fusion(bf16[256,4096]{1,0:T(8,128)(2,1)} %convert_element_type.94, s32[1024]{0:T(1024)S(1)} %iota_add_fusion.3, s32[4096]{0:T(1024)S(1)} %broadcast_add_fusion.6, s32[4096]{0:T(1024)S(1)} %get-tuple-element.421, bf16[4096]{0:T(1024)(128)(2,1)S(1)} %reduce.2, ...), kind=kOutput, calls=%fused_computation.33.clone.1 | convolution fusion | flops 2164523008 | bytes 2674688 | tf_op jit(solution)/shard_map/while/body/eval_jaxpr/dot_general | solution.py:68
  286.2 7.0 %fusion.36 = bf16[256,1024]{0,1:T(8,128)(2,1)S(1)} fusion(bf16[256,4096]{1,0:T(8,128)(2,1)} %convert_element_type.94, s32[1024]{0:T(1024)S(1)} %iota_add_fusion.3, s32[4096]{0:T(1024)S(1)} %broadcast_add_fusion.6, s32[4096]{0:T(1024)S(1)} %get-tuple-element.421, bf16[4096]{0:T(1024)(128)(2,1)S(1)} %reduce.2, ...), kind=kOutput, calls=%fused_computation.33.clone.1 | convolution fusion | flops 2164523008 | bytes 2674688 | tf_op jit(solution)/shard_map/while/body/eval_jaxpr/dot_general | solution.py:68
  297.6 7.0 %fusion.36 = bf16[256,1024]{0,1:T(8,128)(2,1)S(1)} fusion(bf16[256,4096]{1,0:T(8,128)(2,1)} %convert_element_type.94, s32[1024]{0:T(1024)S(1)} %iota_add_fusion.3, s32[4096]{0:T(1024)S(1)} %broadcast_add_fusion.6, s32[4096]{0:T(1024)S(1)} %get-tuple-element.421, bf16[4096]{0:T(1024)(128)(2,1)S(1)} %reduce.2, ...), kind=kOutput, calls=%fused_computation.33.clone.1 | convolution fusion | flops 2164523008 | bytes 2674688 | tf_op jit(solution)/shard_map/while/body/eval_jaxpr/dot_general | solution.py:68
  309.0 7.0 %fusion.36 = bf16[256,1024]{0,1:T(8,128)(2,1)S(1)} fusion(bf16[256,4096]{1,0:T(8,128)(2,1)} %convert_element_type.94, s32[1024]{0:T(1024)S(1)} %iota_add_fusion.3, s32[4096]{0:T(1024)S(1)} %broadcast_add_fusion.6, s32[4096]{0:T(1024)S(1)} %get-tuple-element.421, bf16[4096]{0:T(1024)(128)(2,1)S(1)} %reduce.2, ...), kind=kOutput, calls=%fused_computation.33.clone.1 | convolution fusion | flops 2164523008 | bytes 2674688 | tf_op jit(solution)/shard_map/while/body/eval_jaxpr/dot_general | solution.py:68
  320.4 7.0 %fusion.36 = bf16[256,1024]{0,1:T(8,128)(2,1)S(1)} fusion(bf16[256,4096]{1,0:T(8,128)(2,1)} %convert_element_type.94, s32[1024]{0:T(1024)S(1)} %iota_add_fusion.3, s32[4096]{0:T(1024)S(1)} %broadcast_add_fusion.6, s32[4096]{0:T(1024)S(1)} %get-tuple-element.421, bf16[4096]{0:T(1024)(128)(2,1)S(1)} %reduce.2, ...), kind=kOutput, calls=%fused_computation.33.clone.1 | convolution fusion | flops 2164523008 | bytes 2674688 | tf_op jit(solution)/shard_map/while/body/eval_jaxpr/dot_general | solution.py:68
  328.5 7.2 %reshape.168 = bf16[64,4,8192]{2,1,0:T(4,128)(2,1)} reshape(bf16[256,8192]{1,0:T(8,128)(2,1)} %get-tuple-element.232) | data formatting | bytes 8388608 | tf_op jit(solution)/shard_map/reshape | solution.py:125
  (149 shorter events, 45.1 us)
Async XLA Ops:
  0.6 0.8 copy-start
  1.4 23.1 %copy-start.1 = (f32[4096]{0:T(1024)S(1)}, f32[4096]{0:T(1024)}, u32[]{:S(2)}) copy-start(f32[4096]{0:T(1024)} %param.14) | copy-start | bytes 49156
  24.5 23.1 %copy-start.2 = (s32[4096]{0:T(1024)S(1)}, s32[4096]{0:T(1024)}, u32[]{:S(2)}) copy-start(s32[4096]{0:T(1024)} %param.12) | copy-start | bytes 49156
  47.5 23.1 %copy-start.3 = (s32[4096]{0:T(1024)S(1)}, s32[4096]{0:T(1024)}, u32[]{:S(2)}) copy-start(s32[4096]{0:T(1024)} %param.13) | copy-start | bytes 49156
  149.2 10.4 %copy-start.4 = (f32[4096]{0:T(1024)S(1)}, f32[4096]{0:T(1024)}, u32[]{:S(2)}) copy-start(f32[4096]{0:T(1024)} %param.16) | copy-start | bytes 49156
  151.0 31.7 %all-to-all-start = ((f32[32,64,128]{2,1,0:T(8,128)}), f32[32,64,128]{2,1,0:T(8,128)S(1)}, u32[]{:S(2)}, u32[]{:S(2)}) async-start(f32[32,64,128]{2,1,0:T(8,128)} %copy.13), calls=%async_computation | async-start | bytes 2097152 | tf_op jit(solution)/shard_map/all_to_all | solution.py:18
  182.8 54.5 %copy-start.5 = (f32[64,128]{1,0:T(8,128)}, f32[64,128]{1,0:T(8,128)S(1)}, u32[]{:S(2)}) copy-start(f32[64,128]{1,0:T(8,128)S(1)} %reduce_sum.31) | copy-start | bytes 98308
  184.5 50.3 %all-to-all-start.1 = ((f32[32,64,128]{2,1,0:T(8,128)}), f32[32,64,128]{2,1,0:T(8,128)S(1)}, u32[]{:S(2)}, u32[]{:S(2)}) async-start(f32[32,64,128]{2,1,0:T(8,128)} %broadcast_in_dim.161), calls=%async_computation.1 | async-start | bytes 2097152 | tf_op jit(solution)/shard_map/all_to_all | solution.py:36
where the time goes:
time: 339 us; the launch traced here: 337 us
  local copies, waits for them, and re-layouts  161 us (47%)
  matrix products  98.4 us (29%)
  blocking collectives  42.3 us (12%)
  starting transfers between devices  16 us (5%)
  other arithmetic  15.2 us (4%)
    dot_general x8, matrix products, adjoint_block(): piece = jnp.dot(sources, table, preferred_element_type=jnp.float32)  56.2 us
    psum x4, blocking collectives, by_axis(): x = lax.psum(x, axis)  42.3 us
    dot_general x8, matrix products, forward_block(): along = jnp.dot(flat_fields, table, preferred_element_type=jnp.float32)  42.2 us
    gather x1, local copies, waits for them, and re-layouts, body(): owned_colfrac = col_frac[owner_order]  23 us
    gather x1, local copies, waits for them, and re-layouts, body(): owned_rowfrac = row_frac[owner_order]  23 us
    gather x1, local copies, waits for them, and re-layouts, body(): owned_rows = sensor_rows[owner_order]  23 us
    gather x1, local copies, waits for them, and re-layouts, body(): owned_cols = sensor_cols[owner_order]  23 us
    gather x1, local copies, waits for them, and re-layouts, body(): owned_weights = sensor_weights[owner_order]  23 us
  transfers between devices with their start and end apart: 2, of which 0 were waited for; matrix products, arithmetic and copies ran while one was open for 7% of the time, Pallas kernels for 0%

commit v1 on v0

v1 whole, which is shorter than its diff:
```python
import jax
import jax.numpy as jnp
from jax import lax
from jax.experimental import pallas as pl
from jax.experimental.pallas import tpu as pltpu
from jax.sharding import PartitionSpec as P

F32 = jnp.float32
BF = jnp.bfloat16
I32 = jnp.int32
MESH = pl.DeviceIdType.MESH

OWN = 32
RANK = 16
LIST = OWN * RANK
HALF = LIST // 2


def iota(shape, dim):
    return lax.broadcasted_iota(I32, shape, dim)


def mm(a, b):
    return lax.dot_general(a, b, (((1,), (0,)), ((), ())), preferred_element_type=F32)


def mm_nt(a, b):
    return lax.dot_general(a, b, (((1,), (1,)), ((), ())), preferred_element_type=F32)


def two(x):
    high = x.astype(BF)
    return high, (x - high.astype(F32)).astype(BF)


def mm_two(a, x):
    high, low = two(x)
    return mm(a, high) + mm(a, low)


def table(block, width, col, clo, chi):
    start = block * width
    at = jnp.clip(col - start, -2, width).astype(F32).astype(BF)
    after = jnp.clip(col + 1 - start, -2, width).astype(F32).astype(BF)
    here = iota((width, 128), 0).astype(F32).astype(BF)
    pieces = []
    for t in range(col.shape[1] // 128):
        cut = slice(t * 128, t * 128 + 128)
        low = jnp.where(here == at[:, cut], clo[:, cut], jnp.zeros((), BF))
        pieces.append(jnp.where(here == after[:, cut], chi[:, cut], low))
    return pieces


def row_weights(row, rhi):
    sub = iota((8, row.shape[1]), 0) % 4
    return jnp.where(sub == row, 1.0 - rhi, 0.0) + jnp.where(sub == row + 1, rhi, 0.0)


def times_rows(x, weights8):
    rows, slots = x.shape
    return (x.reshape(rows // 8, 8, slots) * weights8[None]).reshape(rows, slots)


def prep(s, ord_ref, line_ref, rows_ref, cols_ref, rf_ref, cf_ref, w_ref, rscr, rkscr):
    line = line_ref[...]
    onehot = (iota((128, 4096), 0) == (line & 127)).astype(F32).astype(BF)
    found = mm(rows_ref[...].astype(F32).astype(BF), onehot)
    picked = jnp.where(iota((32, 4096), 0) == (line >> 7), found, 0.0)
    slot_rows = jnp.sum(picked, axis=0, keepdims=True)
    for o in range(OWN):
        rscr[o : o + 1, :] = slot_rows[:, o * 128 : o * 128 + 128]
    rows = rscr[...].astype(I32)
    slab = rows >> 2
    upper = (iota((128, 128), 0) < iota((128, 128), 1)).astype(F32).astype(BF)
    sel = []
    for which in range(2):
        mask = slab == s - which
        maskf = jnp.where(mask, 1.0, 0.0)
        rank = mm(maskf.astype(BF), upper)
        rkscr[which] = jnp.where(mask, rank, -1.0)
    lane8 = iota((8, 128), 0).astype(F32)
    for which in range(2):
        for jh in range(2):
            for o in range(OWN):
                sel.append(jnp.where(rkscr[which, o : o + 1, :] == lane8 + 8.0 * jh, 1.0, 0.0))
    sel = jnp.concatenate(sel, axis=0).astype(BF)
    ids = ord_ref[...]
    parts = jnp.concatenate(
        [(ids >> 7).astype(F32), (ids & 127).astype(F32), jnp.ones((32, 128), F32)], axis=0
    ).astype(BF)
    got = mm_nt(parts, sel)
    mine = iota((32, 1024), 0) == ((iota((32, 1024), 1) & 255) >> 3)
    high = jnp.sum(jnp.where(mine, got[0:32], 0.0), axis=0, keepdims=True)
    low = jnp.sum(jnp.where(mine, got[32:64], 0.0), axis=0, keepdims=True)
    valid = jnp.sum(jnp.where(mine, got[64:96], 0.0), axis=0, keepdims=True) > 0.5
    onehot = (iota((128, 1024), 0).astype(F32) == low).astype(F32).astype(BF)
    cols = cols_ref[...]
    rf_hi, rf_lo = two(rf_ref[...])
    w_hi, w_lo = two(w_ref[...])
    cf = cf_ref[...]
    parts = jnp.concatenate(
        [
            (cols >> 7).astype(F32).astype(BF),
            (cols & 127).astype(F32).astype(BF),
            (1.0 - cf).astype(BF),
            cf.astype(BF),
            rf_hi,
            rf_lo,
            w_hi,
            w_lo,
            rows_ref[...].astype(F32).astype(BF),
        ],
        axis=0,
    )
    got = mm(parts, onehot)
    mine = iota((32, 1024), 0).astype(F32) == high
    vals = [
        jnp.sum(jnp.where(mine, got[32 * i : 32 * i + 32], 0.0), axis=0, keepdims=True)
        for i in range(9)
    ]
    rhi = vals[4] + vals[5]
    weight = vals[6] + vals[7]
    grid_row = vals[8].astype(I32) - 4 * s
    second = iota((1, 1024), 1) >= LIST
    use = valid & ((~second) | (grid_row == -1))
    col = jnp.where(use, (vals[0] * 128.0 + vals[1]).astype(I32), -8)
    grid_row = jnp.where(use, grid_row, -8)
    return col, vals[2], vals[3], grid_row, rhi, weight, rows, slab


def expand_matrix():
    a = iota((128, 512), 0)
    b = iota((128, 512), 1)
    return (a == ((b >> 8) * 64 + ((b & 255) >> 2))).astype(F32).astype(BF)


def fields_chunk(xv, first, count):
    return jnp.concatenate([xv[first + i].reshape(256, 128) for i in range(count)], axis=1)


def forward_kernel(
    s_ref, x_ref, ord_ref, line_ref, rows_ref, cols_ref, rf_ref, cf_ref, w_ref,
    out_ref, par_ref, info_ref,
    xv, acc, rscr, rkscr, tab, sem,
):
    s = s_ref[0]
    for c in range(64):
        pltpu.make_async_copy(
            x_ref.at[:, :, pl.ds(c * 128, 128)], xv.at[c], sem.at[c // 8]
        ).start()
    col, clo, chi, grid_row, rhi, weight, rows, slab = prep(
        s, ord_ref, line_ref, rows_ref, cols_ref, rf_ref, cf_ref, w_ref, rscr, rkscr
    )
    par_ref[0:1, :] = col.astype(F32)
    par_ref[1:2, :] = clo
    par_ref[2:3, :] = chi
    par_ref[3:4, :] = grid_row.astype(F32)
    par_ref[4:5, :] = rhi
    par_ref[5:6, :] = weight
    slabf = slab.astype(F32)
    own = jnp.sum(jnp.where(iota((32, 128), 0) == s, slabf, 0.0), axis=0, keepdims=True)
    square = jnp.broadcast_to(own, (128, 128))
    same = (square.T == square) & (iota((128, 128), 0) < iota((128, 128), 1))
    rank = jnp.sum(jnp.where(same, 1.0, 0.0), axis=0, keepdims=True)
    info_ref[0:1, :] = own
    info_ref[1:2, :] = rank

    clo = clo.astype(BF)
    chi = chi.astype(BF)
    acc[...] = jnp.zeros_like(acc)

    def chunk(i, carry):
        for j in range(8):
            pltpu.make_async_copy(
                x_ref.at[:, :, pl.ds(0, 128)], xv.at[8 * i + j], sem.at[i]
            ).wait()
        for j in range(4):
            pieces = table(4 * i + j, 256, col, clo, chi)
            for t in range(8):
                tab[j * 256 : j * 256 + 256, t * 128 : t * 128 + 128] = pieces[t]
        acc[...] += mm(fields_chunk(xv, 8 * i, 8), tab[...])
        return carry

    lax.fori_loop(0, 8, chunk, 0)
    weights8 = row_weights(grid_row, rhi)
    expand = expand_matrix()
    for which in range(2):
        both = []
        for jh in range(2):
            cut = slice(which * LIST + jh * HALF, which * LIST + jh * HALF + HALF)
            both.append(times_rows(acc[:, cut], weights8[:, cut]))
        part = mm_two(expand, jnp.concatenate(both, axis=0))
        out_ref[:, which] = part.T.reshape(OWN, 8, 128)


def exchange_kernel(
    mine, par_ref, info_ref, obs_ref, full_ref, trace_ref,
    box, next_box, prev_box, sums, group, ready, group_ready,
    send_sem, recv_sem, halo_send, halo_recv, sum_send, sum_recv, group_send, group_recv,
):
    s = lax.axis_index("slab")
    z = lax.axis_index("probe")
    after = lax.rem(s + 1, OWN)
    before = lax.rem(s + OWN - 1, OWN)
    barrier = pltpu.get_barrier_semaphore()
    for d in range(1, OWN):
        pl.semaphore_signal(
            barrier, inc=1, device_id={"slab": lax.rem(s + d, OWN)}, device_id_type=MESH
        )
    for d in range(1, 4):
        pl.semaphore_signal(
            barrier, inc=1, device_id={"probe": lax.rem(z + d, 4)}, device_id_type=MESH
        )
    pl.semaphore_wait(barrier, OWN + 2)
    to_next = pltpu.make_async_remote_copy(
        mine.at[:, 0], prev_box, halo_send.at[0], halo_recv.at[0], {"slab": after}, MESH
    )
    to_prev = pltpu.make_async_remote_copy(
        mine.at[:, 1], next_box, halo_send.at[1], halo_recv.at[1], {"slab": before}, MESH
    )
    to_next.start()
    to_prev.start()
    sends = []
    for d in range(1, OWN):
        t = lax.rem(s + d, OWN)
        copy = pltpu.make_async_remote_copy(
            mine.at[t], box.at[s], send_sem.at[d], recv_sem, {"slab": t}, MESH
        )
        copy.start()
        sends.append(copy)
    box[s] = mine[s]
    to_next.wait_recv()
    to_prev.wait_recv()
    own = (mine[:, 0] + next_box[...]).reshape(HALF, 128).T
    bnd = (mine[:, 1] + prev_box[...]).reshape(HALF, 128).T
    full_ref[0] = own
    full_ref[1] = bnd
    weight = par_ref[5:6, 0:LIST]
    square = own * own
    total = jnp.sum(square[0:64] * weight[:, 0:HALF]) + jnp.sum(square[64:128] * weight[:, HALF:LIST])
    ready[...] = jnp.full((8, 128), 1.0, F32) * total
    sum_sends = []
    for d in range(1, OWN):
        t = lax.rem(s + d, OWN)
        copy = pltpu.make_async_remote_copy(
            ready, sums.at[s], sum_send.at[d], sum_recv, {"slab": t}, MESH
        )
        copy.start()
        sum_sends.append(copy)
    sums[s] = ready[...]
    pltpu.make_async_copy(box.at[pl.ds(0, OWN - 1)], box.at[pl.ds(0, OWN - 1)], recv_sem).wait()
    shifted = jnp.concatenate([box[1:OWN, 1], jnp.zeros((1, 8, 128), F32)], axis=0)
    full = (box[:, 0] + shifted).reshape(HALF, 128).T
    slot_slab = info_ref[0:1, :].astype(I32)
    slot_rank = info_ref[1:2, :].astype(I32)
    sub = iota((HALF, 128), 0)
    pick = ((sub >> 3) == slot_slab) & ((sub & 7) == (slot_rank & 7))
    pick = jnp.where(pick, 1.0, 0.0).astype(BF)
    high, low = two(full)
    got = mm(high, pick) + mm(low, pick)
    obs_ref[...] = jnp.where(slot_rank < 8, got[0:64], got[64:128])
    pltpu.make_async_copy(sums.at[pl.ds(0, OWN - 1)], sums.at[pl.ds(0, OWN - 1)], sum_recv).wait()
    group_ready[...] = jnp.sum(sums[...], axis=0)
    group_sends = []
    for d in range(1, 4):
        t = lax.rem(z + d, 4)
        copy = pltpu.make_async_remote_copy(
            group_ready, group.at[z], group_send.at[d], group_recv, {"probe": t}, MESH
        )
        copy.start()
        group_sends.append(copy)
    group[z] = group_ready[...]
    pltpu.make_async_copy(group.at[pl.ds(0, 3)], group.at[pl.ds(0, 3)], group_recv).wait()
    trace_ref[...] = jnp.sum(group[...], axis=0) * (1.0 / 1048576.0)
    to_next.wait_send()
    to_prev.wait_send()
    for copy in sends + sum_sends + group_sends:
        copy.wait_send()


def adjoint_kernel(full_ref, par_ref, out_ref, ov, src, tab, sem):
    col = par_ref[0:1, :].astype(I32)
    clo = par_ref[1:2, :].astype(BF)
    chi = par_ref[2:3, :].astype(BF)
    grid_row = par_ref[3:4, :].astype(I32)
    rhi = par_ref[4:5, :]
    weight = par_ref[5:6, :]
    weights8 = row_weights(grid_row, rhi)
    a = iota((256, 128), 0)
    b = iota((256, 128), 1)
    for which in range(2):
        for jh in range(2):
            cut = slice(which * LIST + jh * HALF, which * LIST + jh * HALF + HALF)
            pick = (b == (jh * 64 + (a >> 2))).astype(F32).astype(BF)
            value = mm_two(pick, full_ref[which] * weight[:, cut])
            src[:, cut] = times_rows(value, weights8[:, cut]).astype(BF)

    def chunk(i, carry):
        for j in range(4):
            pieces = table(4 * i + j, 256, col, clo, chi)
            for t in range(8):
                tab[j, :, t * 128 : t * 128 + 128] = pieces[t]
        for j in range(4):
            got = mm_nt(src[...], tab[j]).astype(BF)
            for h in range(2):
                c = 8 * i + 2 * j + h
                ov[c] = got[:, h * 128 : h * 128 + 128].reshape(64, 4, 128)
                pltpu.make_async_copy(
                    ov.at[c], out_ref.at[:, :, pl.ds(pl.multiple_of(c * 128, 128), 128)], sem
                ).start()
        return carry

    lax.fori_loop(0, 8, chunk, 0)
    pltpu.make_async_copy(ov, ov, sem).wait()


def run_forward(s, fields, rows, cols, rf, cf, w, order):
    vm = pl.BlockSpec(memory_space=pltpu.VMEM)
    sq = lambda x: x.reshape(32, 128)
    return pl.pallas_call(
        forward_kernel,
        out_shape=(
            jax.ShapeDtypeStruct((OWN, 2, 8, 128), F32),
            jax.ShapeDtypeStruct((8, 1024), F32),
            jax.ShapeDtypeStruct((8, 128), F32),
        ),
        in_specs=[pl.BlockSpec(memory_space=pltpu.SMEM), pl.BlockSpec(memory_space=pl.ANY)] + [vm] * 7,
        out_specs=(vm, vm, vm),
        scratch_shapes=[
            pltpu.VMEM((64, 64, 4, 128), BF),
            pltpu.VMEM((256, 1024), F32),
            pltpu.VMEM((32, 128), F32),
            pltpu.VMEM((2, 32, 128), F32),
            pltpu.VMEM((1024, 1024), BF),
            pltpu.SemaphoreType.DMA((8,)),
        ],
        name="forward",
    )(s, fields, sq(order), order.reshape(1, 4096), sq(rows), sq(cols), sq(rf), sq(cf), sq(w))


def run_exchange(mine, par, info):
    vm = pl.BlockSpec(memory_space=pltpu.VMEM)
    dma = pltpu.SemaphoreType.DMA
    return pl.pallas_call(
        exchange_kernel,
        out_shape=(
            jax.ShapeDtypeStruct((64, 128), F32),
            jax.ShapeDtypeStruct((2, 128, HALF), F32),
            jax.ShapeDtypeStruct((8, 128), F32),
        ),
        in_specs=[vm] * 3,
        out_specs=(vm, vm, vm),
        scratch_shapes=[
            pltpu.VMEM((OWN, 2, 8, 128), F32),
            pltpu.VMEM((OWN, 8, 128), F32),
            pltpu.VMEM((OWN, 8, 128), F32),
            pltpu.VMEM((OWN, 8, 128), F32),
            pltpu.VMEM((4, 8, 128), F32),
            pltpu.VMEM((8, 128), F32),
            pltpu.VMEM((8, 128), F32),
            dma((OWN,)), dma, dma((2,)), dma((2,)), dma((OWN,)), dma, dma((4,)), dma,
        ],
        compiler_params=pltpu.CompilerParams(collective_id=0, has_side_effects=True),
        name="exchange",
    )(mine, par, info)


def run_adjoint(full, par):
    vm = pl.BlockSpec(memory_space=pltpu.VMEM)
    return pl.pallas_call(
        adjoint_kernel,
        out_shape=jax.ShapeDtypeStruct((64, 4, 8192), BF),
        in_specs=[vm] * 2,
        out_specs=pl.BlockSpec(memory_space=pl.ANY),
        scratch_shapes=[
            pltpu.VMEM((64, 64, 4, 128), BF),
            pltpu.VMEM((256, 1024), BF),
            pltpu.VMEM((4, 256, 1024), BF),
            pltpu.SemaphoreType.DMA,
        ],
        name="adjoint",
    )(full, par)


def body(fields, rows, cols, rf, cf, w, order):
    s = lax.axis_index("slab").astype(I32).reshape(1)
    mine, par, info = run_forward(s, fields, rows, cols, rf, cf, w, order)
    observed, full, trace = run_exchange(mine, par, info)
    adjoint = run_adjoint(full, par)
    return adjoint, observed, trace[0, 0]


def solution(mesh):
    return jax.shard_map(
        body,
        mesh=mesh,
        in_specs=(P("probe", "slab", None), P(), P(), P(), P(), P(), P()),
        out_specs=(P("probe", "slab", None), P("probe", "slab"), P()),
        check_vma=False,
    )
```

time: 339 us -> 51.8 us (0.15)
  local copies, waits for them, and re-layouts: 161 us -> 1.81 us
  matrix products: 98.4 us -> 0 us
  Pallas kernels: 0 us -> 49 us
  blocking collectives: 42.3 us -> 0 us
  starting transfers between devices: 16 us -> 0 us
  other arithmetic: 15.2 us -> 0 us
    gather x5 -> x0, local copies, waits for them, and re-layouts: 115 us -> none  [the longest x1 23 us: body(): owned_colfrac = col_frac[owner_order]]
    dot_general x16 -> x0, matrix products: 98.4 us -> none  [the longest x8 56.2 us: adjoint_block(): piece = jnp.dot(sources, table, preferred_element_type=jnp.float32)]
    pallas_call x0 -> x3, Pallas kernels: none -> 49 us  [the longest x1 24.8 us: run_exchange(): pl.pallas_call(exchange_kernel, out_shape=(jax.ShapeDtypeStruct((64, 128)...]
    psum x4 -> x0, blocking collectives: 42.3 us -> none  [by_axis(): x = lax.psum(x, axis)]
    convert_element_type x9 -> x0, local copies, waits for them, and re-layouts: 16.2 us -> none  [the longest x8 16.1 us: body(): (spread[:, None, :] * row_weights[None, :, :]).astype(jnp.bfloat16)]
    all_to_all x2 -> x0, starting transfers between devices: 16 us -> none  [the longest x1 8.58 us: summed_on_arrival(): lax.all_to_all(pieces, axis, split_axis=0, concat_axis=0, tiled=True)]
    reshape x10 -> x0, local copies, waits for them, and re-layouts: 15.2 us -> none  [the longest x1 7.16 us: body(): adjoint_sources = result.reshape(probe_count, row_count, width)]
    convert_element_type x25 -> x0, other arithmetic: 9.9 us -> none  [the longest x8 9.25 us: body(): (spread[:, None, :] * row_weights[None, :, :]).astype(jnp.bfloat16)]
  transfers between devices with their start and end apart: 2 -> 0, of which waited for: 0 -> 0; matrix products, arithmetic and copies ran while one was open for 7% -> 0% of each run, Pallas kernels for 0% -> 0%
where the time goes in v1:
time: 51.8 us; the launch traced here: 51.5 us
  Pallas kernels  49 us (95%)
  local copies, waits for them, and re-layouts  1.81 us (3%)
  between operations  0.68 us (1%)
    pallas_call x1, Pallas kernels, run_exchange(): pl.pallas_call(exchange_kernel, out_shape=(jax.ShapeDtypeStruct((64, 128)...  24.8 us
    pallas_call x1, Pallas kernels, run_forward(): pl.pallas_call(forward_kernel, out_shape=(jax.ShapeDtypeStruct((OWN, 2, 8...  12.5 us
    pallas_call x1, Pallas kernels, run_adjoint(): pl.pallas_call(adjoint_kernel, out_shape=jax.ShapeDtypeStruct((64, 4, 819...  11.7 us
    slice x1, local copies, waits for them, and re-layouts, body(): return (adjoint, observed, trace[0, 0])  1.19 us

profile of v1, /device:TPU:1, one launch (start us, length us, event | category | flops | bytes accessed | tf_op | source)
XLA Modules:
  0.0 51.5 jit_solution(8291478439970284491)
XLA Ops:
  0.6 12.5 %forward.1 = (f32[32,2,8,128]{3,2,1,0:T(8,128)}, f32[8,1024]{1,0:T(8,128)}, f32[8,128]{1,0:T(8,128)}) custom-call(s32[1]{0:T(128)} %bitcast.s_ref, bf16[64,4,8192]{2,1,0:T(4,128)(2,1)} %x_ref.1, s32[32,128]{1,0:T(8,128)} %bitcast.9, s32[1,4096]{1,0:T(1,128)} %bitcast.10, s32[32,128]{1,0:T(8,128)} %bitcast.11, s32[32,128]{1,0:T(8,128)} %bitcast.12, ...), custom_call_target="tpu_custom_call" | custom-call | tf_op jit(solution)/shard_map/forward/pallas_call | solution.py:320
  13.1 24.8 %exchange.1 = (f32[64,128]{1,0:T(8,128)}, f32[2,128,256]{2,1,0:T(8,128)}, f32[8,128]{1,0:T(8,128)}) custom-call(f32[32,2,8,128]{3,2,1,0:T(8,128)} %get-tuple-element.9.mine, f32[8,1024]{1,0:T(8,128)} %get-tuple-element.10.par_ref, f32[8,128]{1,0:T(8,128)} %get-tuple-element.11.info_ref), custom_call_target="tpu_custom_call" | custom-call | tf_op jit(solution)/shard_map/exchange/pallas_call | solution.py:344
  37.9 0.0 copy-start
  37.9 1.2 %slice.3 = f32[1,1]{1,0:T(1,128)} slice(f32[8,128]{1,0:T(8,128)} %get-tuple-element.14), slice={[0:1], [0:1]} | slice | bytes 8 | tf_op jit(solution)/shard_map/slice | solution.py:390
  39.1 11.7 %adjoint.1 = bf16[64,4,8192]{2,1,0:T(4,128)(2,1)} custom-call(f32[2,128,256]{2,1,0:T(8,128)} %get-tuple-element.12.full_ref, f32[8,1024]{1,0:T(8,128)} %get-tuple-element.10.par_ref), custom_call_target="tpu_custom_call" | custom-call | tf_op jit(solution)/shard_map/adjoint/pallas_call | solution.py:370
  50.9 0.0 copy-done
  50.9 0.6 %copy.11 = f32[64,128]{1,0:T(8,128)} copy(f32[64,128]{1,0:T(8,128)S(1)} %copy-done) | data formatting | bytes 65536
Async XLA Ops:
  37.9 12.9 %copy-start = (f32[64,128]{1,0:T(8,128)S(1)}, f32[64,128]{1,0:T(8,128)}, u32[]{:S(2)}) copy-start(f32[64,128]{1,0:T(8,128)} %get-tuple-element.19) | copy-start | bytes 98308

commit v2 on v1

v2 whole, which is shorter than its diff:
```python
import jax
import jax.numpy as jnp
from jax import lax
from jax.experimental import pallas as pl
from jax.experimental.pallas import tpu as pltpu
from jax.sharding import PartitionSpec as P

F32 = jnp.float32
BF = jnp.bfloat16
I32 = jnp.int32
MESH = pl.DeviceIdType.MESH

OWN = 32
RANK = 16
LIST = OWN * RANK
HALF = LIST // 2


def iota(shape, dim):
    return lax.broadcasted_iota(I32, shape, dim)


def mm(a, b):
    return lax.dot_general(a, b, (((1,), (0,)), ((), ())), preferred_element_type=F32)


def mm_nt(a, b):
    return lax.dot_general(a, b, (((1,), (1,)), ((), ())), preferred_element_type=F32)


def two(x):
    high = x.astype(BF)
    return high, (x - high.astype(F32)).astype(BF)


def mm_two(a, x):
    high, low = two(x)
    return mm(a, high) + mm(a, low)


def table_rows(block, col, clo, chi):
    after = col + 1
    low = jnp.where((col >> 8) == block, clo, 0.0).astype(BF)
    high = jnp.where((after >> 8) == block, chi, 0.0).astype(BF)
    return low, high


def column_spots(col):
    at = (col & 255).astype(F32).astype(BF)
    after = ((col + 1) & 255).astype(F32).astype(BF)
    return at, after


def row_weights(row, rhi):
    sub = iota((8, row.shape[1]), 0) % 4
    return jnp.where(sub == row, 1.0 - rhi, 0.0) + jnp.where(sub == row + 1, rhi, 0.0)


def times_rows(x, weights8):
    rows, slots = x.shape
    return (x.reshape(rows // 8, 8, slots) * weights8[None]).reshape(rows, slots)


def prep(s, ord_ref, line_ref, rows_ref, cols_ref, rf_ref, cf_ref, w_ref, rscr, rkscr):
    line = line_ref[...]
    onehot = (iota((128, 4096), 0) == (line & 127)).astype(F32).astype(BF)
    found = mm(rows_ref[...].astype(F32).astype(BF), onehot)
    picked = jnp.where(iota((32, 4096), 0) == (line >> 7), found, 0.0)
    slot_rows = jnp.sum(picked, axis=0, keepdims=True)
    for o in range(OWN):
        rscr[o : o + 1, :] = slot_rows[:, o * 128 : o * 128 + 128]
    rows = rscr[...].astype(I32)
    slab = rows >> 2
    upper = (iota((128, 128), 0) < iota((128, 128), 1)).astype(F32).astype(BF)
    sel = []
    for which in range(2):
        mask = slab == s - which
        maskf = jnp.where(mask, 1.0, 0.0)
        rank = mm(maskf.astype(BF), upper)
        rkscr[which] = jnp.where(mask, rank, -1.0)
    lane8 = iota((8, 128), 0).astype(F32)
    for which in range(2):
        for jh in range(2):
            for o in range(OWN):
                sel.append(jnp.where(rkscr[which, o : o + 1, :] == lane8 + 8.0 * jh, 1.0, 0.0))
    sel = jnp.concatenate(sel, axis=0).astype(BF)
    ids = ord_ref[...]
    parts = jnp.concatenate(
        [(ids >> 7).astype(F32), (ids & 127).astype(F32), jnp.ones((32, 128), F32)], axis=0
    ).astype(BF)
    got = mm_nt(parts, sel)
    mine = iota((32, 1024), 0) == ((iota((32, 1024), 1) & 255) >> 3)
    high = jnp.sum(jnp.where(mine, got[0:32], 0.0), axis=0, keepdims=True)
    low = jnp.sum(jnp.where(mine, got[32:64], 0.0), axis=0, keepdims=True)
    valid = jnp.sum(jnp.where(mine, got[64:96], 0.0), axis=0, keepdims=True) > 0.5
    onehot = (iota((128, 1024), 0).astype(F32) == low).astype(F32).astype(BF)
    cols = cols_ref[...]
    rf_hi, rf_lo = two(rf_ref[...])
    w_hi, w_lo = two(w_ref[...])
    cf = cf_ref[...]
    parts = jnp.concatenate(
        [
            (cols >> 7).astype(F32).astype(BF),
            (cols & 127).astype(F32).astype(BF),
            (1.0 - cf).astype(BF),
            cf.astype(BF),
            rf_hi,
            rf_lo,
            w_hi,
            w_lo,
            rows_ref[...].astype(F32).astype(BF),
        ],
        axis=0,
    )
    got = mm(parts, onehot)
    mine = iota((32, 1024), 0).astype(F32) == high
    vals = [
        jnp.sum(jnp.where(mine, got[32 * i : 32 * i + 32], 0.0), axis=0, keepdims=True)
        for i in range(9)
    ]
    rhi = vals[4] + vals[5]
    weight = vals[6] + vals[7]
    grid_row = vals[8].astype(I32) - 4 * s
    second = iota((1, 1024), 1) >= LIST
    use = valid & ((~second) | (grid_row == -1))
    col = jnp.where(use, (vals[0] * 128.0 + vals[1]).astype(I32), -8)
    grid_row = jnp.where(use, grid_row, -8)
    return col, vals[2], vals[3], grid_row, rhi, weight, rows, slab


def expand_matrix():
    a = iota((128, 512), 0)
    b = iota((128, 512), 1)
    return (a == ((b >> 8) * 64 + ((b & 255) >> 2))).astype(F32).astype(BF)


def fields_chunk(xv, first, count):
    return jnp.concatenate([xv[first + i].reshape(256, 128) for i in range(count)], axis=1)


def weighted_source(full, weight, weights8, dst):
    a = iota((256, 128), 0)
    b = iota((256, 128), 1)
    for jh in range(2):
        cut = slice(jh * HALF, jh * HALF + HALF)
        pick = (b == (jh * 64 + (a >> 2))).astype(F32).astype(BF)
        value = mm_two(pick, full * weight[:, cut])
        dst[:, cut] = times_rows(value, weights8[:, cut]).astype(BF)


def main_kernel(
    x_ref, ord_ref, line_ref, rows_ref, cols_ref, rf_ref, cf_ref, w_ref,
    ov, obs_ref, trace_ref,
    xv, acc, tabs, partial, src, rscr, rkscr,
    ordv, linev, rowsv, colsv, rfv, cfv, wv,
    mine_a, mine_b, full_a, next_box, prev_box, box, sums, ready,
    x_sem, in_sem, halo_send, halo_recv, own_send, own_recv, sum_send, sum_recv,
):
    s = lax.axis_index("slab")
    z = lax.axis_index("probe")
    me = s * 4 + z
    small = [
        (ord_ref, ordv), (line_ref, linev), (rows_ref, rowsv), (cols_ref, colsv),
        (rf_ref, rfv), (cf_ref, cfv), (w_ref, wv),
    ]
    small = [pltpu.make_async_copy(a, b, in_sem.at[i]) for i, (a, b) in enumerate(small)]
    for copy in small:
        copy.start()
    for c in range(64):
        pltpu.make_async_copy(
            x_ref.at[:, :, pl.ds(c * 128, 128)], xv.at[c], x_sem.at[c // 8]
        ).start()
    barrier = pltpu.get_barrier_semaphore()

    def greet(d, carry):
        t = lax.rem(me + d, 128)
        pl.semaphore_signal(
            barrier, inc=1, device_id={"slab": t // 4, "probe": lax.rem(t, 4)}, device_id_type=MESH
        )
        return carry

    lax.fori_loop(1, 128, greet, 0)
    for copy in small:
        copy.wait()
    col, clo, chi, grid_row, rhi, weight, rows, slab = prep(
        s, ordv, linev, rowsv, colsv, rfv, cfv, wv, rscr, rkscr
    )
    slabf = slab.astype(F32)
    slot_slab = jnp.sum(jnp.where(iota((32, 128), 0) == s, slabf, 0.0), axis=0, keepdims=True)
    square = jnp.broadcast_to(slot_slab, (128, 128))
    same = (square.T == square) & (iota((128, 128), 0) < iota((128, 128), 1))
    slot_rank = jnp.sum(jnp.where(same, 1.0, 0.0), axis=0, keepdims=True).astype(I32)
    slot_slab = slot_slab.astype(I32)
    weights8 = row_weights(grid_row, rhi)
    here = iota((256, 128), 0).astype(F32).astype(BF)
    expand = expand_matrix()
    zero = jnp.zeros((), BF)

    def forward(which, first):
        cut = slice(which * LIST, which * LIST + LIST)
        at, after = column_spots(col[:, cut])
        acc[...] = jnp.zeros_like(acc)

        def chunk(i, carry):
            if first:
                view = xv.at[pl.ds(8 * i, 8)]
                pltpu.make_async_copy(view, view, x_sem.at[i]).wait()
            for j in range(4):
                low, high = table_rows(4 * i + j, col[:, cut], clo[:, cut], chi[:, cut])
                for t in range(4):
                    c = slice(t * 128, t * 128 + 128)
                    upper = jnp.where(here == after[:, c], high[:, c], zero)
                    tabs[which, 4 * i + j, :, c] = jnp.where(here == at[:, c], low[:, c], upper)
            tab = tabs[which, pl.ds(4 * i, 4)].reshape(1024, LIST)
            acc[...] += mm(fields_chunk(xv, 8 * i, 8), tab)
            return carry

        lax.fori_loop(0, 8, chunk, 0)
        both = []
        for jh in range(2):
            both.append(
                times_rows(
                    acc[:, jh * HALF : jh * HALF + HALF],
                    weights8[:, which * LIST + jh * HALF : which * LIST + jh * HALF + HALF],
                )
            )
        return mm_two(expand, jnp.concatenate(both, axis=0))

    part_b = forward(1, True)
    mine_b[...] = part_b.T.reshape(OWN, 8, 128)
    pl.semaphore_wait(barrier, 127)
    to_prev = pltpu.make_async_remote_copy(
        mine_b, next_box, halo_send.at[0], halo_recv.at[0],
        {"slab": lax.rem(s + OWN - 1, OWN), "probe": z}, MESH,
    )
    to_prev.start()
    part_a = forward(0, False)
    mine_a[...] = part_a.T.reshape(OWN, 8, 128)
    to_next = pltpu.make_async_remote_copy(
        mine_a, prev_box, halo_send.at[1], halo_recv.at[1],
        {"slab": lax.rem(s + 1, OWN), "probe": z}, MESH,
    )
    to_next.start()
    to_prev.wait_recv()
    complete = mine_a[...] + next_box[...]
    full_a[...] = complete
    value_a = complete.reshape(HALF, 128).T
    square = value_a * value_a
    total = jnp.sum(square[0:64] * weight[:, 0:HALF]) + jnp.sum(
        square[64:128] * weight[:, HALF:LIST]
    )
    ready[...] = jnp.full((1, 128), 1.0, F32) * total

    def send_sum(d, carry):
        t = lax.rem(me + d, 128)
        pltpu.make_async_remote_copy(
            ready, sums.at[me], sum_send, sum_recv,
            {"slab": t // 4, "probe": lax.rem(t, 4)}, MESH,
        ).start()
        return carry

    lax.fori_loop(1, 128, send_sum, 0)
    sums[me] = ready[...]

    def send_own(d, carry):
        t = lax.rem(s + d, OWN)
        pltpu.make_async_remote_copy(
            full_a.at[t], box.at[s], own_send, own_recv, {"slab": t, "probe": z}, MESH
        ).start()
        return carry

    lax.fori_loop(1, OWN, send_own, 0)
    box[s] = full_a[s]
    weighted_source(value_a, weight[:, 0:LIST], weights8[:, 0:LIST], src)

    def adjoint_a(i, carry):
        for j in range(4):
            partial[4 * i + j] = mm_nt(src[...], tabs[0, 4 * i + j])
        return carry

    lax.fori_loop(0, 8, adjoint_a, 0)
    to_next.wait_recv()
    value_b = (mine_b[...] + prev_box[...]).reshape(HALF, 128).T
    weighted_source(value_b, weight[:, LIST:], weights8[:, LIST:], src)

    def adjoint_b(i, carry):
        for j in range(4):
            got = (partial[4 * i + j] + mm_nt(src[...], tabs[1, 4 * i + j])).astype(BF)
            for h in range(2):
                ov[8 * i + 2 * j + h] = got[:, h * 128 : h * 128 + 128].reshape(64, 4, 128)
        return carry

    lax.fori_loop(0, 8, adjoint_b, 0)
    view = box.at[pl.ds(0, OWN - 1)]
    pltpu.make_async_copy(view, view, own_recv).wait()
    full = box[...].reshape(HALF, 128).T
    sub = iota((HALF, 128), 0)
    pick = ((sub >> 3) == slot_slab) & ((sub & 7) == (slot_rank & 7))
    pick = jnp.where(pick, 1.0, 0.0).astype(BF)
    high, low = two(full)
    got = mm(high, pick) + mm(low, pick)
    obs_ref[...] = jnp.where(slot_rank < 8, got[0:64], got[64:128])
    view = sums.at[pl.ds(0, 127)]
    pltpu.make_async_copy(view, view, sum_recv).wait()
    trace_ref[...] = jnp.sum(sums[...], axis=0) * (1.0 / 1048576.0)
    to_prev.wait_send()
    to_next.wait_send()
    pltpu.make_async_copy(view, view, sum_send).wait()
    view = box.at[pl.ds(0, OWN - 1)]
    pltpu.make_async_copy(view, view, own_send).wait()


def store_kernel(ov, obs_in, trace_in, out_ref, obs_ref, trace_ref, sem):
    for c in range(64):
        pltpu.make_async_copy(ov.at[c], out_ref.at[:, :, pl.ds(c * 128, 128)], sem).start()
    obs_ref[...] = obs_in[...]
    trace_ref[0, 0] = trace_in[0, 0]
    pltpu.make_async_copy(ov, ov, sem).wait()


def run_main(fields, rows, cols, rf, cf, w, order):
    vm = pl.BlockSpec(memory_space=pltpu.VMEM)
    anywhere = pl.BlockSpec(memory_space=pl.ANY)
    dma = pltpu.SemaphoreType.DMA
    sq = lambda x: x.reshape(32, 128)
    block = pltpu.VMEM((OWN, 8, 128), F32)
    return pl.pallas_call(
        main_kernel,
        out_shape=(
            pltpu.VMEM((64, 64, 4, 128), BF),
            pltpu.VMEM((64, 128), F32),
            pltpu.VMEM((1, 128), F32),
        ),
        in_specs=[anywhere] * 8,
        out_specs=(vm, vm, vm),
        scratch_shapes=[
            pltpu.VMEM((64, 64, 4, 128), BF),
            pltpu.VMEM((256, LIST), F32),
            pltpu.VMEM((2, 32, 256, LIST), BF),
            pltpu.VMEM((32, 256, 256), F32),
            pltpu.VMEM((256, LIST), BF),
            pltpu.VMEM((32, 128), F32),
            pltpu.VMEM((2, 32, 128), F32),
            pltpu.VMEM((32, 128), I32),
            pltpu.VMEM((1, 4096), I32),
            pltpu.VMEM((32, 128), I32),
            pltpu.VMEM((32, 128), I32),
            pltpu.VMEM((32, 128), F32),
            pltpu.VMEM((32, 128), F32),
            pltpu.VMEM((32, 128), F32),
            block, block, block, block, block, block,
            pltpu.VMEM((128, 1, 128), F32),
            pltpu.VMEM((1, 128), F32),
            dma((8,)), dma((7,)), dma((2,)), dma((2,)), dma, dma, dma, dma,
        ],
        compiler_params=pltpu.CompilerParams(
            collective_id=0, has_side_effects=True, vmem_limit_bytes=60000000
        ),
        name="main",
    )(fields, sq(order), order.reshape(1, 4096), sq(rows), sq(cols), sq(rf), sq(cf), sq(w))


def run_store(ov, obs, trace):
    vm = pl.BlockSpec(memory_space=pltpu.VMEM)
    anywhere = pl.BlockSpec(memory_space=pl.ANY)
    return pl.pallas_call(
        store_kernel,
        out_shape=(
            jax.ShapeDtypeStruct((64, 4, 8192), BF),
            jax.ShapeDtypeStruct((64, 128), F32),
            jax.ShapeDtypeStruct((1, 1), F32),
        ),
        in_specs=[vm] * 3,
        out_specs=(anywhere, vm, pl.BlockSpec(memory_space=pltpu.SMEM)),
        scratch_shapes=[pltpu.SemaphoreType.DMA],
        compiler_params=pltpu.CompilerParams(vmem_limit_bytes=8 * 1024 * 1024),
        name="store",
    )(ov, obs, trace)


def body(fields, rows, cols, rf, cf, w, order):
    ov, obs, trace = run_main(fields, rows, cols, rf, cf, w, order)
    adjoint, observed, trace = run_store(ov, obs, trace)
    return adjoint, observed, trace.reshape(())


def solution(mesh):
    return jax.shard_map(
        body,
        mesh=mesh,
        in_specs=(P("probe", "slab", None), P(), P(), P(), P(), P(), P()),
        out_specs=(P("probe", "slab", None), P("probe", "slab"), P()),
        check_vma=False,
    )
```

time: 51.8 us -> 32.1 us (0.62)
  Pallas kernels: 49 us -> 31.3 us
  local copies, waits for them, and re-layouts: 1.81 us -> 0 us
    pallas_call x3 -> x2, Pallas kernels: 49 us -> 31.3 us  [the longest x1 28.7 us: run_main(): pl.pallas_call(main_kernel, out_shape=(pltpu.VMEM((64, 64, 4, 128), BF),...]
    slice x1 -> x0, local copies, waits for them, and re-layouts: 1.19 us -> none  [body(): return (adjoint, observed, trace[0, 0])]
    unnamed x3 -> x0, local copies, waits for them, and re-layouts: 0.62 us -> none
where the time goes in v2:
time: 32.1 us; the launch traced here: 32 us
  Pallas kernels  31.3 us (98%)
  between operations  0.64 us (2%)
    pallas_call x1, Pallas kernels, run_main(): pl.pallas_call(main_kernel, out_shape=(pltpu.VMEM((64, 64, 4, 128), BF),...  28.7 us
    pallas_call x1, Pallas kernels, run_store(): pl.pallas_call(store_kernel, out_shape=(jax.ShapeDtypeStruct((64, 4, 8192...  2.59 us

profile of v2, /device:TPU:1, one launch (start us, length us, event | category | flops | bytes accessed | tf_op | source)
XLA Modules:
  0.0 32.0 jit_solution(4130905191587311358)
XLA Ops:
  0.6 28.7 %main.1 = (bf16[64,64,4,128]{3,2,1,0:T(4,128)(2,1)S(1)}, f32[64,128]{1,0:T(8,128)S(1)}, f32[1,128]{1,0:T(1,128)S(1)}) custom-call(bf16[64,4,8192]{2,1,0:T(4,128)(2,1)} %x_ref.1, s32[32,128]{1,0:T(8,128)} %bitcast.8, s32[1,4096]{1,0:T(1,128)} %bitcast.9, s32[32,128]{1,0:T(8,128)} %bitcast.10, s32[32,128]{1,0:T(8,128)} %bitcast.11, f32[32,128]{1,0:T(8,128)} %bitcast.12, ...), custom_call_target="tpu_custom_call" | custom-call | tf_op jit(solution)/shard_map/main/pallas_call | solution.py:327
  29.4 2.6 %store.1 = (bf16[64,4,8192]{2,1,0:T(4,128)(2,1)}, f32[64,128]{1,0:T(8,128)}, f32[1,1]{1,0:T(1,128)}) custom-call(bf16[64,64,4,128]{3,2,1,0:T(4,128)(2,1)S(1)} %get-tuple-element.9.ov, f32[64,128]{1,0:T(8,128)S(1)} %get-tuple-element.10.obs_in, f32[1,128]{1,0:T(1,128)S(1)} %get-tuple-element.11.trace_in), custom_call_target="tpu_custom_call" | custom-call | tf_op jit(solution)/shard_map/store/pallas_call | solution.py:366

commit v3 on v2

--- a/solution.py
+++ b/solution.py
@@ -38,16 +38,10 @@
     return mm(a, high) + mm(a, low)
 
 
-def table_rows(block, col, clo, chi):
-    after = col + 1
-    low = jnp.where((col >> 8) == block, clo, 0.0).astype(BF)
-    high = jnp.where((after >> 8) == block, chi, 0.0).astype(BF)
-    return low, high
-
-
-def column_spots(col):
-    at = (col & 255).astype(F32).astype(BF)
-    after = ((col + 1) & 255).astype(F32).astype(BF)
+def relative(block, col):
+    start = block * 256
+    at = jnp.clip(col - start, -2, 256).astype(F32).astype(BF)
+    after = jnp.clip(col + 1 - start, -2, 256).astype(F32).astype(BF)
     return at, after
 
 
@@ -135,7 +129,11 @@
 
 
 def fields_chunk(xv, first, count):
-    return jnp.concatenate([xv[first + i].reshape(256, 128) for i in range(count)], axis=1)
+    return jnp.concatenate([xv[first + i] for i in range(count)], axis=1)
+
+
+def table_block(tabs, which, block):
+    return jnp.concatenate([tabs[which, block, t] for t in range(4)], axis=1)
 
 
 def weighted_source(full, weight, weights8, dst):
@@ -153,12 +151,12 @@
     ov, obs_ref, trace_ref,
     xv, acc, tabs, partial, src, rscr, rkscr,
     ordv, linev, rowsv, colsv, rfv, cfv, wv,
-    mine_a, mine_b, full_a, next_box, prev_box, box, sums, ready,
+    mine_a, mine_b, full_a, next_box, prev_box, box, sums, ready, group, group_ready,
     x_sem, in_sem, halo_send, halo_recv, own_send, own_recv, sum_send, sum_recv,
+    group_send, group_recv,
 ):
     s = lax.axis_index("slab")
     z = lax.axis_index("probe")
-    me = s * 4 + z
     small = [
         (ord_ref, ordv), (line_ref, linev), (rows_ref, rowsv), (cols_ref, colsv),
         (rf_ref, rfv), (cf_ref, cfv), (w_ref, wv),
@@ -166,20 +164,25 @@
     small = [pltpu.make_async_copy(a, b, in_sem.at[i]) for i, (a, b) in enumerate(small)]
     for copy in small:
         copy.start()
+    flat = x_ref.reshape(256, 8192)
     for c in range(64):
         pltpu.make_async_copy(
-            x_ref.at[:, :, pl.ds(c * 128, 128)], xv.at[c], x_sem.at[c // 8]
+            flat.at[:, pl.ds(c * 128, 128)], xv.at[c], x_sem.at[c // 32]
         ).start()
     barrier = pltpu.get_barrier_semaphore()
 
     def greet(d, carry):
-        t = lax.rem(me + d, 128)
+        t = lax.rem(s + d, OWN)
         pl.semaphore_signal(
-            barrier, inc=1, device_id={"slab": t // 4, "probe": lax.rem(t, 4)}, device_id_type=MESH
+            barrier, inc=1, device_id={"slab": t, "probe": z}, device_id_type=MESH
         )
         return carry
 
-    lax.fori_loop(1, 128, greet, 0)
+    lax.fori_loop(1, OWN, greet, 0)
+    for d in range(1, 4):
+        pl.semaphore_signal(
+            barrier, inc=1, device_id={"slab": s, "probe": lax.rem(z + d, 4)}, device_id_type=MESH
+        )
     for copy in small:
         copy.wait()
     col, clo, chi, grid_row, rhi, weight, rows, slab = prep(
@@ -198,24 +201,36 @@
 
     def forward(which, first):
         cut = slice(which * LIST, which * LIST + LIST)
-        at, after = column_spots(col[:, cut])
-        acc[...] = jnp.zeros_like(acc)
-
-        def chunk(i, carry):
-            if first:
-                view = xv.at[pl.ds(8 * i, 8)]
-                pltpu.make_async_copy(view, view, x_sem.at[i]).wait()
+        columns = col[:, cut]
+        low = clo[:, cut].astype(BF)
+        high = chi[:, cut].astype(BF)
+
+        def build(i):
             for j in range(4):
-                low, high = table_rows(4 * i + j, col[:, cut], clo[:, cut], chi[:, cut])
+                at, after = relative(4 * i + j, columns)
                 for t in range(4):
                     c = slice(t * 128, t * 128 + 128)
                     upper = jnp.where(here == after[:, c], high[:, c], zero)
-                    tabs[which, 4 * i + j, :, c] = jnp.where(here == at[:, c], low[:, c], upper)
-            tab = tabs[which, pl.ds(4 * i, 4)].reshape(1024, LIST)
-            acc[...] += mm(fields_chunk(xv, 8 * i, 8), tab)
-            return carry
-
-        lax.fori_loop(0, 8, chunk, 0)
+                    tabs[which, 4 * i + j, t] = jnp.where(here == at[:, c], low[:, c], upper)
+
+        def product(i):
+            tab = jnp.concatenate([table_block(tabs, which, 4 * i + j) for j in range(4)], axis=0)
+            return mm(fields_chunk(xv, 8 * i, 8), tab)
+
+        def arrive(i):
+            view = xv.at[pl.ds(32 * i, 32)]
+            pltpu.make_async_copy(view, view, x_sem.at[i]).wait()
+
+        build(0)
+        total = None
+        for i in range(8):
+            if first and i % 4 == 0:
+                arrive(i // 4)
+            if i < 7:
+                build(i + 1)
+            part = product(i)
+            total = part if total is None else total + part
+        acc[...] = total
         both = []
         for jh in range(2):
             both.append(
@@ -228,7 +243,7 @@
 
     part_b = forward(1, True)
     mine_b[...] = part_b.T.reshape(OWN, 8, 128)
-    pl.semaphore_wait(barrier, 127)
+    pl.semaphore_wait(barrier, OWN + 2)
     to_prev = pltpu.make_async_remote_copy(
         mine_b, next_box, halo_send.at[0], halo_recv.at[0],
         {"slab": lax.rem(s + OWN - 1, OWN), "probe": z}, MESH,
@@ -251,16 +266,12 @@
     )
     ready[...] = jnp.full((1, 128), 1.0, F32) * total
 
-    def send_sum(d, carry):
-        t = lax.rem(me + d, 128)
+    for d in range(1, 4):
         pltpu.make_async_remote_copy(
-            ready, sums.at[me], sum_send, sum_recv,
-            {"slab": t // 4, "probe": lax.rem(t, 4)}, MESH,
+            ready, group.at[z], group_send, group_recv,
+            {"slab": s, "probe": lax.rem(z + d, 4)}, MESH,
         ).start()
-        return carry
-
-    lax.fori_loop(1, 128, send_sum, 0)
-    sums[me] = ready[...]
+    group[z] = ready[...]
 
     def send_own(d, carry):
         t = lax.rem(s + d, OWN)
@@ -275,19 +286,32 @@
 
     def adjoint_a(i, carry):
         for j in range(4):
-            partial[4 * i + j] = mm_nt(src[...], tabs[0, 4 * i + j])
+            partial[4 * i + j] = mm_nt(src[...], table_block(tabs, 0, 4 * i + j))
         return carry
 
     lax.fori_loop(0, 8, adjoint_a, 0)
+    view = group.at[pl.ds(0, 3)]
+    pltpu.make_async_copy(view, view, group_recv).wait()
+    group_ready[...] = jnp.sum(group[...], axis=0)
+
+    def send_sum(d, carry):
+        t = lax.rem(s + d, OWN)
+        pltpu.make_async_remote_copy(
+            group_ready, sums.at[s], sum_send, sum_recv, {"slab": t, "probe": z}, MESH
+        ).start()
+        return carry
+
+    lax.fori_loop(1, OWN, send_sum, 0)
+    sums[s] = group_ready[...]
     to_next.wait_recv()
     value_b = (mine_b[...] + prev_box[...]).reshape(HALF, 128).T
     weighted_source(value_b, weight[:, LIST:], weights8[:, LIST:], src)
 
     def adjoint_b(i, carry):
         for j in range(4):
-            got = (partial[4 * i + j] + mm_nt(src[...], tabs[1, 4 * i + j])).astype(BF)
+            got = (partial[4 * i + j] + mm_nt(src[...], table_block(tabs, 1, 4 * i + j))).astype(BF)
             for h in range(2):
-                ov[8 * i + 2 * j + h] = got[:, h * 128 : h * 128 + 128].reshape(64, 4, 128)
+                ov[8 * i + 2 * j + h] = got[:, h * 128 : h * 128 + 128]
         return carry
 
     lax.fori_loop(0, 8, adjoint_b, 0)
@@ -300,19 +324,22 @@
     high, low = two(full)
     got = mm(high, pick) + mm(low, pick)
     obs_ref[...] = jnp.where(slot_rank < 8, got[0:64], got[64:128])
-    view = sums.at[pl.ds(0, 127)]
+    view = sums.at[pl.ds(0, OWN - 1)]
     pltpu.make_async_copy(view, view, sum_recv).wait()
     trace_ref[...] = jnp.sum(sums[...], axis=0) * (1.0 / 1048576.0)
     to_prev.wait_send()
     to_next.wait_send()
     pltpu.make_async_copy(view, view, sum_send).wait()
+    view = group.at[pl.ds(0, 3)]
+    pltpu.make_async_copy(view, view, group_send).wait()
     view = box.at[pl.ds(0, OWN - 1)]
     pltpu.make_async_copy(view, view, own_send).wait()
 
 
 def store_kernel(ov, obs_in, trace_in, out_ref, obs_ref, trace_ref, sem):
+    flat = out_ref.reshape(256, 8192)
     for c in range(64):
-        pltpu.make_async_copy(ov.at[c], out_ref.at[:, :, pl.ds(c * 128, 128)], sem).start()
+        pltpu.make_async_copy(ov.at[c], flat.at[:, pl.ds(c * 128, 128)], sem).start()
     obs_ref[...] = obs_in[...]
     trace_ref[0, 0] = trace_in[0, 0]
     pltpu.make_async_copy(ov, ov, sem).wait()
@@ -327,16 +354,16 @@
     return pl.pallas_call(
         main_kernel,
         out_shape=(
-            pltpu.VMEM((64, 64, 4, 128), BF),
+            pltpu.VMEM((64, 256, 128), BF),
             pltpu.VMEM((64, 128), F32),
             pltpu.VMEM((1, 128), F32),
         ),
         in_specs=[anywhere] * 8,
         out_specs=(vm, vm, vm),
         scratch_shapes=[
-            pltpu.VMEM((64, 64, 4, 128), BF),
+            pltpu.VMEM((64, 256, 128), BF),
             pltpu.VMEM((256, LIST), F32),
-            pltpu.VMEM((2, 32, 256, LIST), BF),
+            pltpu.VMEM((2, 32, 4, 256, 128), BF),
             pltpu.VMEM((32, 256, 256), F32),
             pltpu.VMEM((256, LIST), BF),
             pltpu.VMEM((32, 128), F32),
@@ -349,9 +376,11 @@
             pltpu.VMEM((32, 128), F32),
             pltpu.VMEM((32, 128), F32),
             block, block, block, block, block, block,
-            pltpu.VMEM((128, 1, 128), F32),
+            pltpu.VMEM((OWN, 1, 128), F32),
             pltpu.VMEM((1, 128), F32),
-            dma((8,)), dma((7,)), dma((2,)), dma((2,)), dma, dma, dma, dma,
+            pltpu.VMEM((4, 1, 128), F32),
+            pltpu.VMEM((1, 128), F32),
+            dma((2,)), dma((7,)), dma((2,)), dma((2,)), dma, dma, dma, dma, dma, dma,
         ],
         compiler_params=pltpu.CompilerParams(
             collective_id=0, has_side_effects=True, vmem_limit_bytes=60000000

time: 32.1 us -> 27 us (0.84)
  Pallas kernels: 31.3 us -> 26.2 us
    pallas_call x1, Pallas kernels: 28.7 us -> 23.6 us  [run_main(): pl.pallas_call(main_kernel, out_shape=(pltpu.VMEM((64, 256, 128), BF), pl...]
where the time goes in v3:
time: 27 us; the launch traced here: 26.9 us
  Pallas kernels  26.2 us (97%)
  between operations  0.64 us (2%)
    pallas_call x1, Pallas kernels, run_main(): pl.pallas_call(main_kernel, out_shape=(pltpu.VMEM((64, 256, 128), BF), pl...  23.6 us
    pallas_call x1, Pallas kernels, run_store(): pl.pallas_call(store_kernel, out_shape=(jax.ShapeDtypeStruct((64, 4, 8192...  2.59 us

profile of v3, /device:TPU:1, one launch (start us, length us, event | category | flops | bytes accessed | tf_op | source)
XLA Modules:
  0.0 26.9 jit_solution(12371410530686915732)
XLA Ops:
  0.6 23.6 %main.1 = (bf16[64,256,128]{2,1,0:T(8,128)(2,1)S(1)}, f32[64,128]{1,0:T(8,128)S(1)}, f32[1,128]{1,0:T(1,128)S(1)}) custom-call(bf16[64,4,8192]{2,1,0:T(4,128)(2,1)} %x_ref.1, s32[32,128]{1,0:T(8,128)} %bitcast.8, s32[1,4096]{1,0:T(1,128)} %bitcast.9, s32[32,128]{1,0:T(8,128)} %bitcast.10, s32[32,128]{1,0:T(8,128)} %bitcast.11, f32[32,128]{1,0:T(8,128)} %bitcast.12, ...), custom_call_target="tpu_custom_call" | custom-call | tf_op jit(solution)/shard_map/main/pallas_call | solution.py:354
  24.3 2.6 %store.1 = (bf16[64,4,8192]{2,1,0:T(4,128)(2,1)}, f32[64,128]{1,0:T(8,128)}, f32[1,1]{1,0:T(1,128)}) custom-call(bf16[64,256,128]{2,1,0:T(8,128)(2,1)S(1)} %get-tuple-element.9.ov, f32[64,128]{1,0:T(8,128)S(1)} %get-tuple-element.10.obs_in, f32[1,128]{1,0:T(1,128)S(1)} %get-tuple-element.11.trace_in), custom_call_target="tpu_custom_call" | custom-call | tf_op jit(solution)/shard_map/store/pallas_call | solution.py:395

commit v4 on v3

--- a/solution.py
+++ b/solution.py
@@ -36,13 +36,6 @@
 def mm_two(a, x):
     high, low = two(x)
     return mm(a, high) + mm(a, low)
-
-
-def relative(block, col):
-    start = block * 256
-    at = jnp.clip(col - start, -2, 256).astype(F32).astype(BF)
-    after = jnp.clip(col + 1 - start, -2, 256).astype(F32).astype(BF)
-    return at, after
 
 
 def row_weights(row, rhi):
@@ -122,34 +115,48 @@
     return col, vals[2], vals[3], grid_row, rhi, weight, rows, slab
 
 
-def expand_matrix():
-    a = iota((128, 512), 0)
-    b = iota((128, 512), 1)
-    return (a == ((b >> 8) * 64 + ((b & 255) >> 2))).astype(F32).astype(BF)
+def reduce_matrix():
+    a = iota((512, 128), 0)
+    b = iota((512, 128), 1)
+    return (b == ((a >> 8) * 64 + ((a & 255) >> 2))).astype(F32).astype(BF)
 
 
 def fields_chunk(xv, first, count):
     return jnp.concatenate([xv[first + i] for i in range(count)], axis=1)
 
 
-def table_block(tabs, which, block):
-    return jnp.concatenate([tabs[which, block, t] for t in range(4)], axis=1)
+def spread_out(rows):
+    flat = [r for group in rows for r in group]
+    where = [i for i, group in enumerate(rows) for _ in group]
+    stack = jnp.concatenate([r.astype(F32) for r in flat], axis=0)
+    pad = 16 - len(flat)
+    stack = jnp.concatenate([stack, jnp.zeros((pad, stack.shape[1]), F32)], axis=0).astype(BF)
+    width = 128 * len(rows)
+    a = iota((16, width), 0)
+    group = jnp.full((16, width), -1, I32)
+    for i, g in enumerate(where):
+        group = jnp.where(a == i, g, group)
+    pick = (group == (iota((16, width), 1) >> 7)).astype(F32).astype(BF)
+    out = lax.dot_general(stack, pick, (((0,), (0,)), ((), ())), preferred_element_type=F32)
+    return [out[:, 128 * i : 128 * i + 128] for i in range(len(rows))]
 
 
 def weighted_source(full, weight, weights8, dst):
     a = iota((256, 128), 0)
     b = iota((256, 128), 1)
+    high, low = two(full)
     for jh in range(2):
         cut = slice(jh * HALF, jh * HALF + HALF)
         pick = (b == (jh * 64 + (a >> 2))).astype(F32).astype(BF)
-        value = mm_two(pick, full * weight[:, cut])
+        value = mm_nt(pick, high) + mm_nt(pick, low)
+        value = value * weight[:, cut]
         dst[:, cut] = times_rows(value, weights8[:, cut]).astype(BF)
 
 
 def main_kernel(
     x_ref, ord_ref, line_ref, rows_ref, cols_ref, rf_ref, cf_ref, w_ref,
     ov, obs_ref, trace_ref,
-    xv, acc, tabs, partial, src, rscr, rkscr,
+    xv, reps, tabs, partial, src, rscr, rkscr,
     ordv, linev, rowsv, colsv, rfv, cfv, wv,
     mine_a, mine_b, full_a, next_box, prev_box, box, sums, ready, group, group_ready,
     x_sem, in_sem, halo_send, halo_recv, own_send, own_recv, sum_send, sum_recv,
@@ -164,11 +171,6 @@
     small = [pltpu.make_async_copy(a, b, in_sem.at[i]) for i, (a, b) in enumerate(small)]
     for copy in small:
         copy.start()
-    flat = x_ref.reshape(256, 8192)
-    for c in range(64):
-        pltpu.make_async_copy(
-            flat.at[:, pl.ds(c * 128, 128)], xv.at[c], x_sem.at[c // 32]
-        ).start()
     barrier = pltpu.get_barrier_semaphore()
 
     def greet(d, carry):
@@ -183,6 +185,11 @@
         pl.semaphore_signal(
             barrier, inc=1, device_id={"slab": s, "probe": lax.rem(z + d, 4)}, device_id_type=MESH
         )
+    flat = x_ref.reshape(256, 8192)
+    for c in range(64):
+        pltpu.make_async_copy(
+            flat.at[:, pl.ds(c * 128, 128)], xv.at[c], x_sem.at[c // 32]
+        ).start()
     for copy in small:
         copy.wait()
     col, clo, chi, grid_row, rhi, weight, rows, slab = prep(
@@ -195,62 +202,88 @@
     slot_rank = jnp.sum(jnp.where(same, 1.0, 0.0), axis=0, keepdims=True).astype(I32)
     slot_slab = slot_slab.astype(I32)
     weights8 = row_weights(grid_row, rhi)
-    here = iota((256, 128), 0).astype(F32).astype(BF)
-    expand = expand_matrix()
+    reduce = reduce_matrix()
     zero = jnp.zeros((), BF)
 
-    def forward(which, first):
+    def prepare(which):
         cut = slice(which * LIST, which * LIST + LIST)
         columns = col[:, cut]
-        low = clo[:, cut].astype(BF)
-        high = chi[:, cut].astype(BF)
-
+        rhi_high, rhi_low = two(rhi[:, cut])
+        block, lane, low, high, row, upper = spread_out(
+            [
+                [(columns >> 8).astype(F32).astype(BF)],
+                [(columns & 255).astype(F32).astype(BF)],
+                [clo[:, cut].astype(BF)],
+                [chi[:, cut].astype(BF)],
+                [grid_row[:, cut].astype(F32).astype(BF)],
+                [rhi_high, rhi_low],
+            ]
+        )
+        block, lane, low, high = [
+            jnp.concatenate([x, x], axis=1) for x in (block, lane, low, high)
+        ]
+        here = iota((LIST, 256), 1).astype(F32)
+        reps[which, 0] = block.astype(BF)
+        reps[which, 1] = jnp.where(
+            here == lane, low, jnp.where(here == lane + 1.0, high, 0.0)
+        ).astype(BF)
+        reps[which, 2] = jnp.where((lane == 255.0) & (here == 0.0), high, 0.0).astype(BF)
+        quarter = (iota((LIST, 128), 1) & 3).astype(F32)
+        factor = jnp.where(quarter == row, 1.0 - upper, jnp.where(quarter == row + 1.0, upper, 0.0))
+        return factor
+
+    def forward(which, factor, between):
         def build(i):
-            for j in range(4):
-                at, after = relative(4 * i + j, columns)
-                for t in range(4):
-                    c = slice(t * 128, t * 128 + 128)
-                    upper = jnp.where(here == after[:, c], high[:, c], zero)
-                    tabs[which, 4 * i + j, t] = jnp.where(here == at[:, c], low[:, c], upper)
-
-        def product(i):
-            tab = jnp.concatenate([table_block(tabs, which, 4 * i + j) for j in range(4)], axis=0)
-            return mm(fields_chunk(xv, 8 * i, 8), tab)
+            for g in range(0, LIST, 64):
+                rows = slice(g, g + 64)
+                at = reps[which, 0, rows]
+                inside = reps[which, 1, rows]
+                over = reps[which, 2, rows]
+                for j in range(4):
+                    b = 4 * i + j
+                    tabs[which, b, rows] = jnp.where(
+                        at == b, inside, jnp.where(at == b - 1, over, zero)
+                    )
+
+        def product(i, half):
+            rows = slice(half * HALF, half * HALF + HALF)
+            tab = jnp.concatenate([tabs[which, 4 * i + j, rows] for j in range(4)], axis=1)
+            return mm_nt(tab, fields_chunk(xv, 8 * i, 8))
 
         def arrive(i):
             view = xv.at[pl.ds(32 * i, 32)]
             pltpu.make_async_copy(view, view, x_sem.at[i]).wait()
 
         build(0)
-        total = None
+        total = [None, None]
         for i in range(8):
-            if first and i % 4 == 0:
+            if which == 1 and i % 4 == 0:
                 arrive(i // 4)
             if i < 7:
                 build(i + 1)
-            part = product(i)
-            total = part if total is None else total + part
-        acc[...] = total
+            if i == 4 and between is not None:
+                between()
+            for half in range(2):
+                part = product(i, half)
+                total[half] = part if i == 0 else total[half] + part
         both = []
-        for jh in range(2):
-            both.append(
-                times_rows(
-                    acc[:, jh * HALF : jh * HALF + HALF],
-                    weights8[:, which * LIST + jh * HALF : which * LIST + jh * HALF + HALF],
-                )
-            )
-        return mm_two(expand, jnp.concatenate(both, axis=0))
-
-    part_b = forward(1, True)
-    mine_b[...] = part_b.T.reshape(OWN, 8, 128)
+        for half in range(2):
+            scale = factor[half * HALF : half * HALF + HALF]
+            both.append(total[half] * jnp.concatenate([scale, scale], axis=1))
+        both = jnp.concatenate(both, axis=1)
+        high, low = two(both)
+        return (mm(high, reduce) + mm(low, reduce)).reshape(OWN, 8, 128)
+
+    factor_b = prepare(1)
+    factor_a = []
+    mine_b[...] = forward(1, factor_b, lambda: factor_a.append(prepare(0)))
     pl.semaphore_wait(barrier, OWN + 2)
     to_prev = pltpu.make_async_remote_copy(
         mine_b, next_box, halo_send.at[0], halo_recv.at[0],
         {"slab": lax.rem(s + OWN - 1, OWN), "probe": z}, MESH,
     )
     to_prev.start()
-    part_a = forward(0, False)
-    mine_a[...] = part_a.T.reshape(OWN, 8, 128)
+    mine_a[...] = forward(0, factor_a[0], None)
     to_next = pltpu.make_async_remote_copy(
         mine_a, prev_box, halo_send.at[1], halo_recv.at[1],
         {"slab": lax.rem(s + 1, OWN), "probe": z}, MESH,
@@ -259,10 +292,12 @@
     to_prev.wait_recv()
     complete = mine_a[...] + next_box[...]
     full_a[...] = complete
-    value_a = complete.reshape(HALF, 128).T
-    square = value_a * value_a
-    total = jnp.sum(square[0:64] * weight[:, 0:HALF]) + jnp.sum(
-        square[64:128] * weight[:, HALF:LIST]
+    value_a = complete.reshape(HALF, 128)
+    side = (iota((8, 128), 0) == (iota((8, 128), 1) >> 6)).astype(F32).astype(BF)
+    high, low = two(value_a * value_a)
+    squares = mm_nt(side, high) + mm_nt(side, low)
+    total = jnp.sum(
+        squares[0:1] * weight[:, 0:HALF] + squares[1:2] * weight[:, HALF:LIST]
     )
     ready[...] = jnp.full((1, 128), 1.0, F32) * total
 
@@ -286,7 +321,7 @@
 
     def adjoint_a(i, carry):
         for j in range(4):
-            partial[4 * i + j] = mm_nt(src[...], table_block(tabs, 0, 4 * i + j))
+            partial[4 * i + j] = mm(src[...], tabs[0, 4 * i + j])
         return carry
 
     lax.fori_loop(0, 8, adjoint_a, 0)
@@ -304,14 +339,13 @@
     lax.fori_loop(1, OWN, send_sum, 0)
     sums[s] = group_ready[...]
     to_next.wait_recv()
-    value_b = (mine_b[...] + prev_box[...]).reshape(HALF, 128).T
+    value_b = (mine_b[...] + prev_box[...]).reshape(HALF, 128)
     weighted_source(value_b, weight[:, LIST:], weights8[:, LIST:], src)
 
     def adjoint_b(i, carry):
         for j in range(4):
-            got = (partial[4 * i + j] + mm_nt(src[...], table_block(tabs, 1, 4 * i + j))).astype(BF)
-            for h in range(2):
-                ov[8 * i + 2 * j + h] = got[:, h * 128 : h * 128 + 128]
+            got = (partial[4 * i + j] + mm(src[...], tabs[1, 4 * i + j])).astype(BF)
+            ov[4 * i + j] = got
         return carry
 
     lax.fori_loop(0, 8, adjoint_b, 0)
@@ -339,7 +373,8 @@
 def store_kernel(ov, obs_in, trace_in, out_ref, obs_ref, trace_ref, sem):
     flat = out_ref.reshape(256, 8192)
     for c in range(64):
-        pltpu.make_async_copy(ov.at[c], flat.at[:, pl.ds(c * 128, 128)], sem).start()
+        half = ov.at[c // 2, :, pl.ds((c % 2) * 128, 128)]
+        pltpu.make_async_copy(half, flat.at[:, pl.ds(c * 128, 128)], sem).start()
     obs_ref[...] = obs_in[...]
     trace_ref[0, 0] = trace_in[0, 0]
     pltpu.make_async_copy(ov, ov, sem).wait()
@@ -354,7 +389,7 @@
     return pl.pallas_call(
         main_kernel,
         out_shape=(
-            pltpu.VMEM((64, 256, 128), BF),
+            pltpu.VMEM((32, 256, 256), BF),
             pltpu.VMEM((64, 128), F32),
             pltpu.VMEM((1, 128), F32),
         ),
@@ -362,8 +397,8 @@
         out_specs=(vm, vm, vm),
         scratch_shapes=[
             pltpu.VMEM((64, 256, 128), BF),
-            pltpu.VMEM((256, LIST), F32),
-            pltpu.VMEM((2, 32, 4, 256, 128), BF),
+            pltpu.VMEM((2, 3, LIST, 256), BF),
+            pltpu.VMEM((2, 32, LIST, 256), BF),
             pltpu.VMEM((32, 256, 256), F32),
             pltpu.VMEM((256, LIST), BF),
             pltpu.VMEM((32, 128), F32),

time: 27 us -> 25.7 us (0.952)
  Pallas kernels: 26.2 us -> 24.9 us
    pallas_call x1, Pallas kernels: 23.6 us -> 22.3 us  [run_main(): pl.pallas_call(main_kernel, out_shape=(pltpu.VMEM((32, 256, 256), BF), pl...]
where the time goes in v4:
time: 25.7 us; the launch traced here: 25.5 us
  Pallas kernels  24.9 us (97%)
  between operations  0.64 us (2%)
    pallas_call x1, Pallas kernels, run_main(): pl.pallas_call(main_kernel, out_shape=(pltpu.VMEM((32, 256, 256), BF), pl...  22.3 us
    pallas_call x1, Pallas kernels, run_store(): pl.pallas_call(store_kernel, out_shape=(jax.ShapeDtypeStruct((64, 4, 8192...  2.59 us

profile of v4, /device:TPU:1, one launch (start us, length us, event | category | flops | bytes accessed | tf_op | source)
XLA Modules:
  0.0 25.5 jit_solution(8837879769775808548)
XLA Ops:
  0.6 22.3 %main.1 = (bf16[32,256,256]{2,1,0:T(8,128)(2,1)S(1)}, f32[64,128]{1,0:T(8,128)S(1)}, f32[1,128]{1,0:T(1,128)S(1)}) custom-call(bf16[64,4,8192]{2,1,0:T(4,128)(2,1)} %x_ref.1, s32[32,128]{1,0:T(8,128)} %bitcast.8, s32[1,4096]{1,0:T(1,128)} %bitcast.9, s32[32,128]{1,0:T(8,128)} %bitcast.10, s32[32,128]{1,0:T(8,128)} %bitcast.11, f32[32,128]{1,0:T(8,128)} %bitcast.12, ...), custom_call_target="tpu_custom_call" | custom-call | tf_op jit(solution)/shard_map/main/pallas_call | solution.py:389
  22.9 2.6 %store.1 = (bf16[64,4,8192]{2,1,0:T(4,128)(2,1)}, f32[64,128]{1,0:T(8,128)}, f32[1,1]{1,0:T(1,128)}) custom-call(bf16[32,256,256]{2,1,0:T(8,128)(2,1)S(1)} %get-tuple-element.9.ov, f32[64,128]{1,0:T(8,128)S(1)} %get-tuple-element.10.obs_in, f32[1,128]{1,0:T(1,128)S(1)} %get-tuple-element.11.trace_in), custom_call_target="tpu_custom_call" | custom-call | tf_op jit(solution)/shard_map/store/pallas_call | solution.py:430

commit v5 on v4

--- a/solution.py
+++ b/solution.py
@@ -153,14 +153,24 @@
         dst[:, cut] = times_rows(value, weights8[:, cut]).astype(BF)
 
 
+def far_first():
+    hops = lambda d: min(d, 4 - d)
+    steps = [
+        (y, x, c, z) for y in range(4) for x in range(4) for c in range(2) for z in range(4)
+    ][1:]
+    return sorted(steps, key=lambda d: -(hops(d[0]) + hops(d[1]) + hops(d[3])))
+
+
+STEPS = far_first()
+
+
 def main_kernel(
     x_ref, ord_ref, line_ref, rows_ref, cols_ref, rf_ref, cf_ref, w_ref,
     ov, obs_ref, trace_ref,
     xv, reps, tabs, partial, src, rscr, rkscr,
     ordv, linev, rowsv, colsv, rfv, cfv, wv,
-    mine_a, mine_b, full_a, next_box, prev_box, box, sums, ready, group, group_ready,
+    mine_a, mine_b, full_a, next_box, prev_box, box, sums, ready,
     x_sem, in_sem, halo_send, halo_recv, own_send, own_recv, sum_send, sum_recv,
-    group_send, group_recv,
 ):
     s = lax.axis_index("slab")
     z = lax.axis_index("probe")
@@ -173,18 +183,18 @@
         copy.start()
     barrier = pltpu.get_barrier_semaphore()
 
-    def greet(d, carry):
-        t = lax.rem(s + d, OWN)
-        pl.semaphore_signal(
-            barrier, inc=1, device_id={"slab": t, "probe": z}, device_id_type=MESH
-        )
-        return carry
-
-    lax.fori_loop(1, OWN, greet, 0)
-    for d in range(1, 4):
-        pl.semaphore_signal(
-            barrier, inc=1, device_id={"slab": s, "probe": lax.rem(z + d, 4)}, device_id_type=MESH
-        )
+    place = (s // 8, lax.rem(s // 2, 4), lax.rem(s, 2), z)
+    moved = [
+        [lax.rem(at + d, length) for d in range(length)]
+        for at, length in zip(place, (4, 4, 2, 4))
+    ]
+
+    def other(step):
+        y, x, core, level = (m[d] for m, d in zip(moved, step))
+        return {"slab": y * 8 + x * 2 + core, "probe": level}
+
+    for step in STEPS:
+        pl.semaphore_signal(barrier, inc=1, device_id=other(step), device_id_type=MESH)
     flat = x_ref.reshape(256, 8192)
     for c in range(64):
         pltpu.make_async_copy(
@@ -277,7 +287,7 @@
     factor_b = prepare(1)
     factor_a = []
     mine_b[...] = forward(1, factor_b, lambda: factor_a.append(prepare(0)))
-    pl.semaphore_wait(barrier, OWN + 2)
+    pl.semaphore_wait(barrier, 127)
     to_prev = pltpu.make_async_remote_copy(
         mine_b, next_box, halo_send.at[0], halo_recv.at[0],
         {"slab": lax.rem(s + OWN - 1, OWN), "probe": z}, MESH,
@@ -301,54 +311,33 @@
     )
     ready[...] = jnp.full((1, 128), 1.0, F32) * total
 
-    for d in range(1, 4):
+    me = s * 4 + z
+    for step in STEPS:
         pltpu.make_async_remote_copy(
-            ready, group.at[z], group_send, group_recv,
-            {"slab": s, "probe": lax.rem(z + d, 4)}, MESH,
+            ready, sums.at[me], sum_send, sum_recv, other(step), MESH
         ).start()
-    group[z] = ready[...]
-
-    def send_own(d, carry):
+    sums[me] = ready[...]
+    to_prev.wait_send()
+
+    def send_own(d):
         t = lax.rem(s + d, OWN)
         pltpu.make_async_remote_copy(
             full_a.at[t], box.at[s], own_send, own_recv, {"slab": t, "probe": z}, MESH
         ).start()
-        return carry
-
-    lax.fori_loop(1, OWN, send_own, 0)
+
     box[s] = full_a[s]
     weighted_source(value_a, weight[:, 0:LIST], weights8[:, 0:LIST], src)
 
-    def adjoint_a(i, carry):
-        for j in range(4):
-            partial[4 * i + j] = mm(src[...], tabs[0, 4 * i + j])
-        return carry
-
-    lax.fori_loop(0, 8, adjoint_a, 0)
-    view = group.at[pl.ds(0, 3)]
-    pltpu.make_async_copy(view, view, group_recv).wait()
-    group_ready[...] = jnp.sum(group[...], axis=0)
-
-    def send_sum(d, carry):
-        t = lax.rem(s + d, OWN)
-        pltpu.make_async_remote_copy(
-            group_ready, sums.at[s], sum_send, sum_recv, {"slab": t, "probe": z}, MESH
-        ).start()
-        return carry
-
-    lax.fori_loop(1, OWN, send_sum, 0)
-    sums[s] = group_ready[...]
+    for i in range(32):
+        partial[i] = mm(src[...], tabs[0, i])
+        if i < OWN - 1:
+            send_own(i + 1)
     to_next.wait_recv()
     value_b = (mine_b[...] + prev_box[...]).reshape(HALF, 128)
     weighted_source(value_b, weight[:, LIST:], weights8[:, LIST:], src)
 
-    def adjoint_b(i, carry):
-        for j in range(4):
-            got = (partial[4 * i + j] + mm(src[...], tabs[1, 4 * i + j])).astype(BF)
-            ov[4 * i + j] = got
-        return carry
-
-    lax.fori_loop(0, 8, adjoint_b, 0)
+    for i in range(32):
+        ov[i] = (partial[i] + mm(src[...], tabs[1, i])).astype(BF)
     view = box.at[pl.ds(0, OWN - 1)]
     pltpu.make_async_copy(view, view, own_recv).wait()
     full = box[...].reshape(HALF, 128).T
@@ -358,14 +347,11 @@
     high, low = two(full)
     got = mm(high, pick) + mm(low, pick)
     obs_ref[...] = jnp.where(slot_rank < 8, got[0:64], got[64:128])
-    view = sums.at[pl.ds(0, OWN - 1)]
+    view = sums.at[pl.ds(0, 127)]
     pltpu.make_async_copy(view, view, sum_recv).wait()
     trace_ref[...] = jnp.sum(sums[...], axis=0) * (1.0 / 1048576.0)
-    to_prev.wait_send()
     to_next.wait_send()
     pltpu.make_async_copy(view, view, sum_send).wait()
-    view = group.at[pl.ds(0, 3)]
-    pltpu.make_async_copy(view, view, group_send).wait()
     view = box.at[pl.ds(0, OWN - 1)]
     pltpu.make_async_copy(view, view, own_send).wait()
 
@@ -411,11 +397,9 @@
             pltpu.VMEM((32, 128), F32),
             pltpu.VMEM((32, 128), F32),
             block, block, block, block, block, block,
-            pltpu.VMEM((OWN, 1, 128), F32),
+            pltpu.VMEM((128, 1, 128), F32),
             pltpu.VMEM((1, 128), F32),
-            pltpu.VMEM((4, 1, 128), F32),
-            pltpu.VMEM((1, 128), F32),
-            dma((2,)), dma((7,)), dma((2,)), dma((2,)), dma, dma, dma, dma, dma, dma,
+            dma((2,)), dma((7,)), dma((2,)), dma((2,)), dma, dma, dma, dma,
         ],
         compiler_params=pltpu.CompilerParams(
             collective_id=0, has_side_effects=True, vmem_limit_bytes=60000000

time: 25.7 us -> 26.7 us (1.039)
  Pallas kernels: 24.9 us -> 26 us
    pallas_call x1, Pallas kernels: 22.3 us -> 23.4 us  [run_main(): pl.pallas_call(main_kernel, out_shape=(pltpu.VMEM((32, 256, 256), BF), pl...]
where the time goes in v5:
time: 26.7 us; the launch traced here: 26.6 us
  Pallas kernels  26 us (97%)
  between operations  0.64 us (2%)
    pallas_call x1, Pallas kernels, run_main(): pl.pallas_call(main_kernel, out_shape=(pltpu.VMEM((32, 256, 256), BF), pl...  23.4 us
    pallas_call x1, Pallas kernels, run_store(): pl.pallas_call(store_kernel, out_shape=(jax.ShapeDtypeStruct((64, 4, 8192...  2.59 us

profile of v5, /device:TPU:1, one launch (start us, length us, event | category | flops | bytes accessed | tf_op | source)
XLA Modules:
  0.0 26.6 jit_solution(13852259366957908010)
XLA Ops:
  0.6 23.4 %main.1 = (bf16[32,256,256]{2,1,0:T(8,128)(2,1)S(1)}, f32[64,128]{1,0:T(8,128)S(1)}, f32[1,128]{1,0:T(1,128)S(1)}) custom-call(bf16[64,4,8192]{2,1,0:T(4,128)(2,1)} %x_ref.1, s32[32,128]{1,0:T(8,128)} %bitcast.8, s32[1,4096]{1,0:T(1,128)} %bitcast.9, s32[32,128]{1,0:T(8,128)} %bitcast.10, s32[32,128]{1,0:T(8,128)} %bitcast.11, f32[32,128]{1,0:T(8,128)} %bitcast.12, ...), custom_call_target="tpu_custom_call" | custom-call | tf_op jit(solution)/shard_map/main/pallas_call | solution.py:375
  24.0 2.6 %store.1 = (bf16[64,4,8192]{2,1,0:T(4,128)(2,1)}, f32[64,128]{1,0:T(8,128)}, f32[1,1]{1,0:T(1,128)}) custom-call(bf16[32,256,256]{2,1,0:T(8,128)(2,1)S(1)} %get-tuple-element.9.ov, f32[64,128]{1,0:T(8,128)S(1)} %get-tuple-element.10.obs_in, f32[1,128]{1,0:T(1,128)S(1)} %get-tuple-element.11.trace_in), custom_call_target="tpu_custom_call" | custom-call | tf_op jit(solution)/shard_map/store/pallas_call | solution.py:414

commit v6 on v5

--- a/solution.py
+++ b/solution.py
@@ -155,10 +155,8 @@
 
 def far_first():
     hops = lambda d: min(d, 4 - d)
-    steps = [
-        (y, x, c, z) for y in range(4) for x in range(4) for c in range(2) for z in range(4)
-    ][1:]
-    return sorted(steps, key=lambda d: -(hops(d[0]) + hops(d[1]) + hops(d[3])))
+    steps = [(y, x, c) for y in range(4) for x in range(4) for c in range(2)][1:]
+    return sorted(steps, key=lambda d: -(hops(d[0]) + hops(d[1])))
 
 
 STEPS = far_first()
@@ -169,8 +167,9 @@
     ov, obs_ref, trace_ref,
     xv, reps, tabs, partial, src, rscr, rkscr,
     ordv, linev, rowsv, colsv, rfv, cfv, wv,
-    mine_a, mine_b, full_a, next_box, prev_box, box, sums, ready,
+    mine_a, mine_b, full_a, next_box, prev_box, box, sums, ready, group, group_ready,
     x_sem, in_sem, halo_send, halo_recv, own_send, own_recv, sum_send, sum_recv,
+    group_send, group_recv,
 ):
     s = lax.axis_index("slab")
     z = lax.axis_index("probe")
@@ -183,22 +182,25 @@
         copy.start()
     barrier = pltpu.get_barrier_semaphore()
 
-    place = (s // 8, lax.rem(s // 2, 4), lax.rem(s, 2), z)
+    place = (s // 8, lax.rem(s // 2, 4), lax.rem(s, 2))
     moved = [
-        [lax.rem(at + d, length) for d in range(length)]
-        for at, length in zip(place, (4, 4, 2, 4))
+        [lax.rem(at + d, length) for d in range(length)] for at, length in zip(place, (4, 4, 2))
     ]
 
     def other(step):
-        y, x, core, level = (m[d] for m, d in zip(moved, step))
-        return {"slab": y * 8 + x * 2 + core, "probe": level}
-
-    for step in STEPS:
-        pl.semaphore_signal(barrier, inc=1, device_id=other(step), device_id_type=MESH)
+        y, x, core = (m[d] for m, d in zip(moved, step))
+        return y * 8 + x * 2 + core
+
+    slabs = [other(step) for step in STEPS]
+    levels = [lax.rem(z + d, 4) for d in (2, 1, 3)]
+    for t in slabs:
+        pl.semaphore_signal(barrier, inc=1, device_id={"slab": t, "probe": z}, device_id_type=MESH)
+    for t in levels:
+        pl.semaphore_signal(barrier, inc=1, device_id={"slab": s, "probe": t}, device_id_type=MESH)
     flat = x_ref.reshape(256, 8192)
     for c in range(64):
         pltpu.make_async_copy(
-            flat.at[:, pl.ds(c * 128, 128)], xv.at[c], x_sem.at[c // 32]
+            flat.at[:, pl.ds(c * 128, 128)], xv.at[c], x_sem
         ).start()
     for copy in small:
         copy.wait()
@@ -242,64 +244,83 @@
         factor = jnp.where(quarter == row, 1.0 - upper, jnp.where(quarter == row + 1.0, upper, 0.0))
         return factor
 
-    def forward(which, factor, between):
-        def build(i):
-            for g in range(0, LIST, 64):
-                rows = slice(g, g + 64)
-                at = reps[which, 0, rows]
-                inside = reps[which, 1, rows]
-                over = reps[which, 2, rows]
-                for j in range(4):
-                    b = 4 * i + j
-                    tabs[which, b, rows] = jnp.where(
-                        at == b, inside, jnp.where(at == b - 1, over, zero)
-                    )
+    def forward(which, factor, between, mine, done):
+        def pieces(half):
+            return [slice(jh * HALF + half * 128, jh * HALF + half * 128 + 128) for jh in range(2)]
+
+        def build(i, half):
+            for piece in pieces(half):
+                for g in (piece.start, piece.start + 64):
+                    rows = slice(g, g + 64)
+                    at = reps[which, 0, rows]
+                    inside = reps[which, 1, rows]
+                    over = reps[which, 2, rows]
+                    for j in range(4):
+                        b = 4 * i + j
+                        tabs[which, b, rows] = jnp.where(
+                            at == b, inside, jnp.where(at == b - 1, over, zero)
+                        )
 
         def product(i, half):
-            rows = slice(half * HALF, half * HALF + HALF)
-            tab = jnp.concatenate([tabs[which, 4 * i + j, rows] for j in range(4)], axis=1)
+            tab = jnp.concatenate(
+                [
+                    jnp.concatenate([tabs[which, 4 * i + j, rows] for rows in pieces(half)], axis=0)
+                    for j in range(4)
+                ],
+                axis=1,
+            )
             return mm_nt(tab, fields_chunk(xv, 8 * i, 8))
 
-        def arrive(i):
-            view = xv.at[pl.ds(32 * i, 32)]
-            pltpu.make_async_copy(view, view, x_sem.at[i]).wait()
-
-        build(0)
-        total = [None, None]
-        for i in range(8):
-            if which == 1 and i % 4 == 0:
-                arrive(i // 4)
-            if i < 7:
-                build(i + 1)
-            if i == 4 and between is not None:
-                between()
-            for half in range(2):
-                part = product(i, half)
-                total[half] = part if i == 0 else total[half] + part
-        both = []
+        build(0, 0)
+        build(4, 0)
+        if which == 1:
+            pltpu.make_async_copy(xv, xv, x_sem).wait()
         for half in range(2):
-            scale = factor[half * HALF : half * HALF + HALF]
-            both.append(total[half] * jnp.concatenate([scale, scale], axis=1))
-        both = jnp.concatenate(both, axis=1)
-        high, low = two(both)
-        return (mm(high, reduce) + mm(low, reduce)).reshape(OWN, 8, 128)
+            total = [None, None]
+            for i in range(4):
+                if i < 3:
+                    build(i + 1, half)
+                    build(i + 5, half)
+                elif half == 0:
+                    build(0, 1)
+                    build(4, 1)
+                if half == 1 and i == 1 and between is not None:
+                    between()
+                for k in range(2):
+                    part = product(i + 4 * k, half)
+                    total[k] = part if i == 0 else total[k] + part
+            both = []
+            for jh, piece in enumerate(pieces(half)):
+                scale = jnp.concatenate([factor[piece]] * 2, axis=1)
+                rows = slice(jh * 128, jh * 128 + 128)
+                both.append(total[0][rows] * scale + total[1][rows] * scale)
+            high, low = two(jnp.concatenate(both, axis=1))
+            mine[16 * half : 16 * half + 16] = (mm(high, reduce) + mm(low, reduce)).reshape(16, 8, 128)
+            done(half)
+
+    def send_half(mine, box_there, link, t, half):
+        rows = pl.ds(16 * half, 16)
+        return pltpu.make_async_remote_copy(
+            mine.at[rows], box_there.at[rows], halo_send.at[link, half], halo_recv.at[link, half],
+            {"slab": t, "probe": z}, MESH,
+        )
+
+    after = lax.rem(s + 1, OWN)
+    before = lax.rem(s + OWN - 1, OWN)
+    to_prev = [send_half(mine_b, next_box, 0, before, half) for half in range(2)]
+    to_next = [send_half(mine_a, prev_box, 1, after, half) for half in range(2)]
+
+    def done_b(half):
+        if half == 0:
+            pl.semaphore_wait(barrier, OWN + 2)
+        to_prev[half].start()
 
     factor_b = prepare(1)
     factor_a = []
-    mine_b[...] = forward(1, factor_b, lambda: factor_a.append(prepare(0)))
-    pl.semaphore_wait(barrier, 127)
-    to_prev = pltpu.make_async_remote_copy(
-        mine_b, next_box, halo_send.at[0], halo_recv.at[0],
-        {"slab": lax.rem(s + OWN - 1, OWN), "probe": z}, MESH,
-    )
-    to_prev.start()
-    mine_a[...] = forward(0, factor_a[0], None)
-    to_next = pltpu.make_async_remote_copy(
-        mine_a, prev_box, halo_send.at[1], halo_recv.at[1],
-        {"slab": lax.rem(s + 1, OWN), "probe": z}, MESH,
-    )
-    to_next.start()
-    to_prev.wait_recv()
+    forward(1, factor_b, lambda: factor_a.append(prepare(0)), mine_b, done_b)
+    forward(0, factor_a[0], None, mine_a, lambda half: to_next[half].start())
+    for copy in to_prev:
+        copy.wait_recv()
     complete = mine_a[...] + next_box[...]
     full_a[...] = complete
     value_a = complete.reshape(HALF, 128)
@@ -311,28 +332,32 @@
     )
     ready[...] = jnp.full((1, 128), 1.0, F32) * total
 
-    me = s * 4 + z
-    for step in STEPS:
+    for t in levels:
         pltpu.make_async_remote_copy(
-            ready, sums.at[me], sum_send, sum_recv, other(step), MESH
+            ready, group.at[z], group_send, group_recv, {"slab": s, "probe": t}, MESH
         ).start()
-    sums[me] = ready[...]
-    to_prev.wait_send()
-
-    def send_own(d):
-        t = lax.rem(s + d, OWN)
+    group[z] = ready[...]
+    for t in slabs:
         pltpu.make_async_remote_copy(
             full_a.at[t], box.at[s], own_send, own_recv, {"slab": t, "probe": z}, MESH
         ).start()
-
+    for copy in to_prev:
+        copy.wait_send()
     box[s] = full_a[s]
     weighted_source(value_a, weight[:, 0:LIST], weights8[:, 0:LIST], src)
 
     for i in range(32):
         partial[i] = mm(src[...], tabs[0, i])
-        if i < OWN - 1:
-            send_own(i + 1)
-    to_next.wait_recv()
+    view = group.at[pl.ds(0, 3)]
+    pltpu.make_async_copy(view, view, group_recv).wait()
+    group_ready[...] = jnp.sum(group[...], axis=0)
+    for t in slabs:
+        pltpu.make_async_remote_copy(
+            group_ready, sums.at[s], sum_send, sum_recv, {"slab": t, "probe": z}, MESH
+        ).start()
+    sums[s] = group_ready[...]
+    for copy in to_next:
+        copy.wait_recv()
     value_b = (mine_b[...] + prev_box[...]).reshape(HALF, 128)
     weighted_source(value_b, weight[:, LIST:], weights8[:, LIST:], src)
 
@@ -347,11 +372,14 @@
     high, low = two(full)
     got = mm(high, pick) + mm(low, pick)
     obs_ref[...] = jnp.where(slot_rank < 8, got[0:64], got[64:128])
-    view = sums.at[pl.ds(0, 127)]
+    view = sums.at[pl.ds(0, OWN - 1)]
     pltpu.make_async_copy(view, view, sum_recv).wait()
     trace_ref[...] = jnp.sum(sums[...], axis=0) * (1.0 / 1048576.0)
-    to_next.wait_send()
+    for copy in to_next:
+        copy.wait_send()
     pltpu.make_async_copy(view, view, sum_send).wait()
+    view = group.at[pl.ds(0, 3)]
+    pltpu.make_async_copy(view, view, group_send).wait()
     view = box.at[pl.ds(0, OWN - 1)]
     pltpu.make_async_copy(view, view, own_send).wait()
 
@@ -397,9 +425,11 @@
             pltpu.VMEM((32, 128), F32),
             pltpu.VMEM((32, 128), F32),
             block, block, block, block, block, block,
-            pltpu.VMEM((128, 1, 128), F32),
+            pltpu.VMEM((OWN, 1, 128), F32),
             pltpu.VMEM((1, 128), F32),
-            dma((2,)), dma((7,)), dma((2,)), dma((2,)), dma, dma, dma, dma,
+            pltpu.VMEM((4, 1, 128), F32),
+            pltpu.VMEM((1, 128), F32),
+            dma, dma((7,)), dma((2, 2)), dma((2, 2)), dma, dma, dma, dma, dma, dma,
         ],
         compiler_params=pltpu.CompilerParams(
             collective_id=0, has_side_effects=True, vmem_limit_bytes=60000000

time: 26.7 us -> 27.1 us (1.015)
  Pallas kernels: 26 us -> 26.3 us
    pallas_call x1, Pallas kernels: 23.4 us -> 23.7 us  [run_main(): pl.pallas_call(main_kernel, out_shape=(pltpu.VMEM((32, 256, 256), BF), pl...]
where the time goes in v6:
time: 27.1 us; the launch traced here: 26.9 us
  Pallas kernels  26.3 us (97%)
  between operations  0.64 us (2%)
    pallas_call x1, Pallas kernels, run_main(): pl.pallas_call(main_kernel, out_shape=(pltpu.VMEM((32, 256, 256), BF), pl...  23.7 us
    pallas_call x1, Pallas kernels, run_store(): pl.pallas_call(store_kernel, out_shape=(jax.ShapeDtypeStruct((64, 4, 8192...  2.59 us

profile of v6, /device:TPU:1, one launch (start us, length us, event | category | flops | bytes accessed | tf_op | source)
XLA Modules:
  0.0 26.9 jit_solution(7693415831322051937)
XLA Ops:
  0.6 23.7 %main.1 = (bf16[32,256,256]{2,1,0:T(8,128)(2,1)S(1)}, f32[64,128]{1,0:T(8,128)S(1)}, f32[1,128]{1,0:T(1,128)S(1)}) custom-call(bf16[64,4,8192]{2,1,0:T(4,128)(2,1)} %x_ref.1, s32[32,128]{1,0:T(8,128)} %bitcast.8, s32[1,4096]{1,0:T(1,128)} %bitcast.9, s32[32,128]{1,0:T(8,128)} %bitcast.10, s32[32,128]{1,0:T(8,128)} %bitcast.11, f32[32,128]{1,0:T(8,128)} %bitcast.12, ...), custom_call_target="tpu_custom_call" | custom-call | tf_op jit(solution)/shard_map/main/pallas_call | solution.py:403
  24.3 2.6 %store.1 = (bf16[64,4,8192]{2,1,0:T(4,128)(2,1)}, f32[64,128]{1,0:T(8,128)}, f32[1,1]{1,0:T(1,128)}) custom-call(bf16[32,256,256]{2,1,0:T(8,128)(2,1)S(1)} %get-tuple-element.9.ov, f32[64,128]{1,0:T(8,128)S(1)} %get-tuple-element.10.obs_in, f32[1,128]{1,0:T(1,128)S(1)} %get-tuple-element.11.trace_in), custom_call_target="tpu_custom_call" | custom-call | tf_op jit(solution)/shard_map/store/pallas_call | solution.py:444

commit v7 on v5

--- a/solution.py
+++ b/solution.py
@@ -162,6 +162,7 @@
 
 
 STEPS = far_first()
+FAR = 71
 
 
 def main_kernel(
@@ -170,7 +171,7 @@
     xv, reps, tabs, partial, src, rscr, rkscr,
     ordv, linev, rowsv, colsv, rfv, cfv, wv,
     mine_a, mine_b, full_a, next_box, prev_box, box, sums, ready,
-    x_sem, in_sem, halo_send, halo_recv, own_send, own_recv, sum_send, sum_recv,
+    x_sem, in_sem, halo_send, halo_recv, own_send, own_recv, sum_send, sum_recv, plane,
 ):
     s = lax.axis_index("slab")
     z = lax.axis_index("probe")
@@ -180,7 +181,12 @@
     ]
     small = [pltpu.make_async_copy(a, b, in_sem.at[i]) for i, (a, b) in enumerate(small)]
     for copy in small:
-        copy.start()
+        copy.start(priority=1)
+    flat = x_ref.reshape(256, 8192)
+    for c in range(64):
+        pltpu.make_async_copy(
+            flat.at[:, pl.ds(c * 128, 128)], xv.at[c], x_sem.at[c // 32]
+        ).start()
     barrier = pltpu.get_barrier_semaphore()
 
     place = (s // 8, lax.rem(s // 2, 4), lax.rem(s, 2), z)
@@ -193,13 +199,9 @@
         y, x, core, level = (m[d] for m, d in zip(moved, step))
         return {"slab": y * 8 + x * 2 + core, "probe": level}
 
-    for step in STEPS:
+    near = [step for step in STEPS if step[3] == 0 or step[:3] == (0, 0, 0)]
+    for step in near:
         pl.semaphore_signal(barrier, inc=1, device_id=other(step), device_id_type=MESH)
-    flat = x_ref.reshape(256, 8192)
-    for c in range(64):
-        pltpu.make_async_copy(
-            flat.at[:, pl.ds(c * 128, 128)], xv.at[c], x_sem.at[c // 32]
-        ).start()
     for copy in small:
         copy.wait()
     col, clo, chi, grid_row, rhi, weight, rows, slab = prep(
@@ -287,7 +289,11 @@
     factor_b = prepare(1)
     factor_a = []
     mine_b[...] = forward(1, factor_b, lambda: factor_a.append(prepare(0)))
-    pl.semaphore_wait(barrier, 127)
+    pl.semaphore_wait(barrier, OWN + 2)
+    for d in range(1, 4):
+        pl.semaphore_signal(
+            plane, inc=1, device_id={"slab": s, "probe": lax.rem(z + d, 4)}, device_id_type=MESH
+        )
     to_prev = pltpu.make_async_remote_copy(
         mine_b, next_box, halo_send.at[0], halo_recv.at[0],
         {"slab": lax.rem(s + OWN - 1, OWN), "probe": z}, MESH,
@@ -312,26 +318,30 @@
     ready[...] = jnp.full((1, 128), 1.0, F32) * total
 
     me = s * 4 + z
-    for step in STEPS:
+    pl.semaphore_wait(plane, 3)
+
+    def send_sum(step):
         pltpu.make_async_remote_copy(
             ready, sums.at[me], sum_send, sum_recv, other(step), MESH
         ).start()
+
+    for step in STEPS[:FAR]:
+        send_sum(step)
     sums[me] = ready[...]
-    to_prev.wait_send()
-
-    def send_own(d):
-        t = lax.rem(s + d, OWN)
-        pltpu.make_async_remote_copy(
-            full_a.at[t], box.at[s], own_send, own_recv, {"slab": t, "probe": z}, MESH
-        ).start()
-
+    for step in near:
+        if step[3] == 0:
+            there = other(step)
+            pltpu.make_async_remote_copy(
+                full_a.at[there["slab"]], box.at[s], own_send, own_recv, there, MESH
+            ).start()
     box[s] = full_a[s]
     weighted_source(value_a, weight[:, 0:LIST], weights8[:, 0:LIST], src)
+    to_prev.wait_send()
 
     for i in range(32):
         partial[i] = mm(src[...], tabs[0, i])
-        if i < OWN - 1:
-            send_own(i + 1)
+        for step in STEPS[FAR + 2 * i : FAR + 2 * i + 2]:
+            send_sum(step)
     to_next.wait_recv()
     value_b = (mine_b[...] + prev_box[...]).reshape(HALF, 128)
     weighted_source(value_b, weight[:, LIST:], weights8[:, LIST:], src)
@@ -399,7 +409,7 @@
             block, block, block, block, block, block,
             pltpu.VMEM((128, 1, 128), F32),
             pltpu.VMEM((1, 128), F32),
-            dma((2,)), dma((7,)), dma((2,)), dma((2,)), dma, dma, dma, dma,
+            dma((2,)), dma((7,)), dma((2,)), dma((2,)), dma, dma, dma, dma, pltpu.SemaphoreType.REGULAR,
         ],
         compiler_params=pltpu.CompilerParams(
             collective_id=0, has_side_effects=True, vmem_limit_bytes=60000000

time: 26.7 us -> 27.1 us (1.015)
  Pallas kernels: 26 us -> 26.3 us
    pallas_call x1, Pallas kernels: 23.4 us -> 23.7 us  [run_main(): pl.pallas_call(main_kernel, out_shape=(pltpu.VMEM((32, 256, 256), BF), pl...]
where the time goes in v7:
time: 27.1 us; the launch traced here: 26.9 us
  Pallas kernels  26.3 us (97%)
  between operations  0.64 us (2%)
    pallas_call x1, Pallas kernels, run_main(): pl.pallas_call(main_kernel, out_shape=(pltpu.VMEM((32, 256, 256), BF), pl...  23.7 us
    pallas_call x1, Pallas kernels, run_store(): pl.pallas_call(store_kernel, out_shape=(jax.ShapeDtypeStruct((64, 4, 8192...  2.59 us

profile of v7, /device:TPU:1, one launch (start us, length us, event | category | flops | bytes accessed | tf_op | source)
XLA Modules:
  0.0 26.9 jit_solution(13001583326876202868)
XLA Ops:
  0.6 23.7 %main.1 = (bf16[32,256,256]{2,1,0:T(8,128)(2,1)S(1)}, f32[64,128]{1,0:T(8,128)S(1)}, f32[1,128]{1,0:T(1,128)S(1)}) custom-call(bf16[64,4,8192]{2,1,0:T(4,128)(2,1)} %x_ref.1, s32[32,128]{1,0:T(8,128)} %bitcast.8, s32[1,4096]{1,0:T(1,128)} %bitcast.9, s32[32,128]{1,0:T(8,128)} %bitcast.10, s32[32,128]{1,0:T(8,128)} %bitcast.11, f32[32,128]{1,0:T(8,128)} %bitcast.12, ...), custom_call_target="tpu_custom_call" | custom-call | tf_op jit(solution)/shard_map/main/pallas_call | solution.py:385
  24.3 2.6 %store.1 = (bf16[64,4,8192]{2,1,0:T(4,128)(2,1)}, f32[64,128]{1,0:T(8,128)}, f32[1,1]{1,0:T(1,128)}) custom-call(bf16[32,256,256]{2,1,0:T(8,128)(2,1)S(1)} %get-tuple-element.9.ov, f32[64,128]{1,0:T(8,128)S(1)} %get-tuple-element.10.obs_in, f32[1,128]{1,0:T(1,128)S(1)} %get-tuple-element.11.trace_in), custom_call_target="tpu_custom_call" | custom-call | tf_op jit(solution)/shard_map/store/pallas_call | solution.py:424

commit v8 on v7

--- a/solution.py
+++ b/solution.py
@@ -162,7 +162,6 @@
 
 
 STEPS = far_first()
-FAR = 71
 
 
 def main_kernel(
@@ -181,27 +180,27 @@
     ]
     small = [pltpu.make_async_copy(a, b, in_sem.at[i]) for i, (a, b) in enumerate(small)]
     for copy in small:
-        copy.start(priority=1)
+        copy.start()
+    barrier = pltpu.get_barrier_semaphore()
+
+    place = (s // 8, lax.rem(s // 2, 4), lax.rem(s, 2), z)
+    moved = [
+        [lax.rem(at + d, length) for d in range(length)]
+        for at, length in zip(place, (4, 4, 2, 4))
+    ]
+
+    def other(step):
+        y, x, core, level = (m[d] for m, d in zip(moved, step))
+        return {"slab": y * 8 + x * 2 + core, "probe": level}
+
+    near = [step for step in STEPS if step[3] == 0 or step[:3] == (0, 0, 0)]
+    for step in near:
+        pl.semaphore_signal(barrier, inc=1, device_id=other(step), device_id_type=MESH)
     flat = x_ref.reshape(256, 8192)
     for c in range(64):
         pltpu.make_async_copy(
             flat.at[:, pl.ds(c * 128, 128)], xv.at[c], x_sem.at[c // 32]
         ).start()
-    barrier = pltpu.get_barrier_semaphore()
-
-    place = (s // 8, lax.rem(s // 2, 4), lax.rem(s, 2), z)
-    moved = [
-        [lax.rem(at + d, length) for d in range(length)]
-        for at, length in zip(place, (4, 4, 2, 4))
-    ]
-
-    def other(step):
-        y, x, core, level = (m[d] for m, d in zip(moved, step))
-        return {"slab": y * 8 + x * 2 + core, "probe": level}
-
-    near = [step for step in STEPS if step[3] == 0 or step[:3] == (0, 0, 0)]
-    for step in near:
-        pl.semaphore_signal(barrier, inc=1, device_id=other(step), device_id_type=MESH)
     for copy in small:
         copy.wait()
     col, clo, chi, grid_row, rhi, weight, rows, slab = prep(
@@ -325,7 +324,7 @@
             ready, sums.at[me], sum_send, sum_recv, other(step), MESH
         ).start()
 
-    for step in STEPS[:FAR]:
+    for step in STEPS:
         send_sum(step)
     sums[me] = ready[...]
     for step in near:
@@ -340,8 +339,6 @@
 
     for i in range(32):
         partial[i] = mm(src[...], tabs[0, i])
-        for step in STEPS[FAR + 2 * i : FAR + 2 * i + 2]:
-            send_sum(step)
     to_next.wait_recv()
     value_b = (mine_b[...] + prev_box[...]).reshape(HALF, 128)
     weighted_source(value_b, weight[:, LIST:], weights8[:, LIST:], src)

time: 27.1 us -> 24.9 us (0.919)
  Pallas kernels: 26.3 us -> 24 us
    pallas_call x1, Pallas kernels: 23.7 us -> 21.4 us  [run_main(): pl.pallas_call(main_kernel, out_shape=(pltpu.VMEM((32, 256, 256), BF), pl...]
where the time goes in v8:
time: 24.9 us; the launch traced here: 24.7 us
  Pallas kernels  24 us (96%)
  between operations  0.64 us (3%)
    pallas_call x1, Pallas kernels, run_main(): pl.pallas_call(main_kernel, out_shape=(pltpu.VMEM((32, 256, 256), BF), pl...  21.4 us
    pallas_call x1, Pallas kernels, run_store(): pl.pallas_call(store_kernel, out_shape=(jax.ShapeDtypeStruct((64, 4, 8192...  2.59 us

profile of v8, /device:TPU:1, one launch (start us, length us, event | category | flops | bytes accessed | tf_op | source)
XLA Modules:
  0.0 24.7 jit_solution(10178409431263771157)
XLA Ops:
  0.6 21.4 %main.1 = (bf16[32,256,256]{2,1,0:T(8,128)(2,1)S(1)}, f32[64,128]{1,0:T(8,128)S(1)}, f32[1,128]{1,0:T(1,128)S(1)}) custom-call(bf16[64,4,8192]{2,1,0:T(4,128)(2,1)} %x_ref.1, s32[32,128]{1,0:T(8,128)} %bitcast.8, s32[1,4096]{1,0:T(1,128)} %bitcast.9, s32[32,128]{1,0:T(8,128)} %bitcast.10, s32[32,128]{1,0:T(8,128)} %bitcast.11, f32[32,128]{1,0:T(8,128)} %bitcast.12, ...), custom_call_target="tpu_custom_call" | custom-call | tf_op jit(solution)/shard_map/main/pallas_call | solution.py:382
  22.1 2.6 %store.1 = (bf16[64,4,8192]{2,1,0:T(4,128)(2,1)}, f32[64,128]{1,0:T(8,128)}, f32[1,1]{1,0:T(1,128)}) custom-call(bf16[32,256,256]{2,1,0:T(8,128)(2,1)S(1)} %get-tuple-element.9.ov, f32[64,128]{1,0:T(8,128)S(1)} %get-tuple-element.10.obs_in, f32[1,128]{1,0:T(1,128)S(1)} %get-tuple-element.11.trace_in), custom_call_target="tpu_custom_call" | custom-call | tf_op jit(solution)/shard_map/store/pallas_call | solution.py:421

commit v9 on v8

--- a/solution.py
+++ b/solution.py
@@ -344,7 +344,8 @@
     weighted_source(value_b, weight[:, LIST:], weights8[:, LIST:], src)
 
     for i in range(32):
-        ov[i] = (partial[i] + mm(src[...], tabs[1, i])).astype(BF)
+        got = (partial[i] + mm(src[...], tabs[1, i])).astype(BF)
+        ov[:, :, 256 * i : 256 * i + 256] = got.reshape(64, 4, 256)
     view = box.at[pl.ds(0, OWN - 1)]
     pltpu.make_async_copy(view, view, own_recv).wait()
     full = box[...].reshape(HALF, 128).T
@@ -364,10 +365,9 @@
 
 
 def store_kernel(ov, obs_in, trace_in, out_ref, obs_ref, trace_ref, sem):
-    flat = out_ref.reshape(256, 8192)
-    for c in range(64):
-        half = ov.at[c // 2, :, pl.ds((c % 2) * 128, 128)]
-        pltpu.make_async_copy(half, flat.at[:, pl.ds(c * 128, 128)], sem).start()
+    for c in range(8):
+        rows = pl.ds(8 * c, 8)
+        pltpu.make_async_copy(ov.at[rows], out_ref.at[rows], sem).start()
     obs_ref[...] = obs_in[...]
     trace_ref[0, 0] = trace_in[0, 0]
     pltpu.make_async_copy(ov, ov, sem).wait()
@@ -382,7 +382,7 @@
     return pl.pallas_call(
         main_kernel,
         out_shape=(
-            pltpu.VMEM((32, 256, 256), BF),
+            pltpu.VMEM((64, 4, 8192), BF),
             pltpu.VMEM((64, 128), F32),
             pltpu.VMEM((1, 128), F32),
         ),

time: 24.9 us -> 24.9 us (level)
  no operation moved by 1% of the time
where the time goes in v9:
time: 24.9 us; the launch traced here: 24.7 us
  Pallas kernels  24.1 us (97%)
  between operations  0.64 us (3%)
    pallas_call x1, Pallas kernels, run_main(): pl.pallas_call(main_kernel, out_shape=(pltpu.VMEM((64, 4, 8192), BF), plt...  21.4 us
    pallas_call x1, Pallas kernels, run_store(): pl.pallas_call(store_kernel, out_shape=(jax.ShapeDtypeStruct((64, 4, 8192...  2.63 us

profile of v9, /device:TPU:1, one launch (start us, length us, event | category | flops | bytes accessed | tf_op | source)
XLA Modules:
  0.0 24.7 jit_solution(15538635775187237418)
XLA Ops:
  0.6 21.4 %main.1 = (bf16[64,4,8192]{2,1,0:T(4,128)(2,1)S(1)}, f32[64,128]{1,0:T(8,128)S(1)}, f32[1,128]{1,0:T(1,128)S(1)}) custom-call(bf16[64,4,8192]{2,1,0:T(4,128)(2,1)} %x_ref.1, s32[32,128]{1,0:T(8,128)} %bitcast.8, s32[1,4096]{1,0:T(1,128)} %bitcast.9, s32[32,128]{1,0:T(8,128)} %bitcast.10, s32[32,128]{1,0:T(8,128)} %bitcast.11, f32[32,128]{1,0:T(8,128)} %bitcast.12, ...), custom_call_target="tpu_custom_call" | custom-call | tf_op jit(solution)/shard_map/main/pallas_call | solution.py:382
  22.1 2.6 %store.1 = (bf16[64,4,8192]{2,1,0:T(4,128)(2,1)}, f32[64,128]{1,0:T(8,128)}, f32[1,1]{1,0:T(1,128)}) custom-call(bf16[64,4,8192]{2,1,0:T(4,128)(2,1)S(1)} %get-tuple-element.9.ov, f32[64,128]{1,0:T(8,128)S(1)} %get-tuple-element.10.obs_in, f32[1,128]{1,0:T(1,128)S(1)} %get-tuple-element.11.trace_in), custom_call_target="tpu_custom_call" | custom-call | tf_op jit(solution)/shard_map/store/pallas_call | solution.py:421

commit v10 on v9

--- a/solution.py
+++ b/solution.py
@@ -166,7 +166,7 @@
 
 def main_kernel(
     x_ref, ord_ref, line_ref, rows_ref, cols_ref, rf_ref, cf_ref, w_ref,
-    ov, obs_ref, trace_ref,
+    ov, box_ref, info_ref, trace_ref,
     xv, reps, tabs, partial, src, rscr, rkscr,
     ordv, linev, rowsv, colsv, rfv, cfv, wv,
     mine_a, mine_b, full_a, next_box, prev_box, box, sums, ready,
@@ -206,12 +206,6 @@
     col, clo, chi, grid_row, rhi, weight, rows, slab = prep(
         s, ordv, linev, rowsv, colsv, rfv, cfv, wv, rscr, rkscr
     )
-    slabf = slab.astype(F32)
-    slot_slab = jnp.sum(jnp.where(iota((32, 128), 0) == s, slabf, 0.0), axis=0, keepdims=True)
-    square = jnp.broadcast_to(slot_slab, (128, 128))
-    same = (square.T == square) & (iota((128, 128), 0) < iota((128, 128), 1))
-    slot_rank = jnp.sum(jnp.where(same, 1.0, 0.0), axis=0, keepdims=True).astype(I32)
-    slot_slab = slot_slab.astype(I32)
     weights8 = row_weights(grid_row, rhi)
     reduce = reduce_matrix()
     zero = jnp.zeros((), BF)
@@ -311,11 +305,8 @@
     side = (iota((8, 128), 0) == (iota((8, 128), 1) >> 6)).astype(F32).astype(BF)
     high, low = two(value_a * value_a)
     squares = mm_nt(side, high) + mm_nt(side, low)
-    total = jnp.sum(
-        squares[0:1] * weight[:, 0:HALF] + squares[1:2] * weight[:, HALF:LIST]
-    )
-    ready[...] = jnp.full((1, 128), 1.0, F32) * total
-
+    lanes = squares[0:1] * weight[:, 0:HALF] + squares[1:2] * weight[:, HALF:LIST]
+    ready[...] = lanes[:, 0:128] + lanes[:, 128:256]
     me = s * 4 + z
     pl.semaphore_wait(plane, 3)
 
@@ -335,6 +326,13 @@
             ).start()
     box[s] = full_a[s]
     weighted_source(value_a, weight[:, 0:LIST], weights8[:, 0:LIST], src)
+    slabf = (rscr[...].astype(I32) >> 2).astype(F32)
+    slot_slab = jnp.sum(jnp.where(iota((32, 128), 0) == s, slabf, 0.0), axis=0, keepdims=True)
+    square = jnp.broadcast_to(slot_slab, (128, 128))
+    same = (square.T == square) & (iota((128, 128), 0) < iota((128, 128), 1))
+    slot_rank = jnp.sum(jnp.where(same, 1.0, 0.0), axis=0, keepdims=True)
+    info_ref[0:1] = slot_slab
+    info_ref[1:2] = slot_rank
     to_prev.wait_send()
 
     for i in range(32):
@@ -348,13 +346,7 @@
         ov[:, :, 256 * i : 256 * i + 256] = got.reshape(64, 4, 256)
     view = box.at[pl.ds(0, OWN - 1)]
     pltpu.make_async_copy(view, view, own_recv).wait()
-    full = box[...].reshape(HALF, 128).T
-    sub = iota((HALF, 128), 0)
-    pick = ((sub >> 3) == slot_slab) & ((sub & 7) == (slot_rank & 7))
-    pick = jnp.where(pick, 1.0, 0.0).astype(BF)
-    high, low = two(full)
-    got = mm(high, pick) + mm(low, pick)
-    obs_ref[...] = jnp.where(slot_rank < 8, got[0:64], got[64:128])
+    box_ref[...] = box[...]
     view = sums.at[pl.ds(0, 127)]
     pltpu.make_async_copy(view, view, sum_recv).wait()
     trace_ref[...] = jnp.sum(sums[...], axis=0) * (1.0 / 1048576.0)
@@ -364,12 +356,20 @@
     pltpu.make_async_copy(view, view, own_send).wait()
 
 
-def store_kernel(ov, obs_in, trace_in, out_ref, obs_ref, trace_ref, sem):
+def store_kernel(ov, box, info, trace_in, out_ref, obs_ref, trace_ref, sem):
     for c in range(8):
         rows = pl.ds(8 * c, 8)
         pltpu.make_async_copy(ov.at[rows], out_ref.at[rows], sem).start()
-    obs_ref[...] = obs_in[...]
-    trace_ref[0, 0] = trace_in[0, 0]
+    full = box[...].reshape(HALF, 128).T
+    slot_slab = info[0:1].astype(I32)
+    slot_rank = info[1:2].astype(I32)
+    sub = iota((HALF, 128), 0)
+    pick = ((sub >> 3) == slot_slab) & ((sub & 7) == (slot_rank & 7))
+    pick = jnp.where(pick, 1.0, 0.0).astype(BF)
+    high, low = two(full)
+    got = mm(high, pick) + mm(low, pick)
+    obs_ref[...] = jnp.where(slot_rank < 8, got[0:64], got[64:128])
+    trace_ref[0, 0] = jnp.sum(trace_in[...])
     pltpu.make_async_copy(ov, ov, sem).wait()
 
 
@@ -383,11 +383,12 @@
         main_kernel,
         out_shape=(
             pltpu.VMEM((64, 4, 8192), BF),
-            pltpu.VMEM((64, 128), F32),
+            pltpu.VMEM((OWN, 8, 128), F32),
+            pltpu.VMEM((8, 128), F32),
             pltpu.VMEM((1, 128), F32),
         ),
         in_specs=[anywhere] * 8,
-        out_specs=(vm, vm, vm),
+        out_specs=(vm, vm, vm, vm),
         scratch_shapes=[
             pltpu.VMEM((64, 256, 128), BF),
             pltpu.VMEM((2, 3, LIST, 256), BF),
@@ -415,7 +416,7 @@
     )(fields, sq(order), order.reshape(1, 4096), sq(rows), sq(cols), sq(rf), sq(cf), sq(w))
 
 
-def run_store(ov, obs, trace):
+def run_store(ov, box, info, trace):
     vm = pl.BlockSpec(memory_space=pltpu.VMEM)
     anywhere = pl.BlockSpec(memory_space=pl.ANY)
     return pl.pallas_call(
@@ -425,17 +426,17 @@
             jax.ShapeDtypeStruct((64, 128), F32),
             jax.ShapeDtypeStruct((1, 1), F32),
         ),
-        in_specs=[vm] * 3,
+        in_specs=[vm] * 4,
         out_specs=(anywhere, vm, pl.BlockSpec(memory_space=pltpu.SMEM)),
         scratch_shapes=[pltpu.SemaphoreType.DMA],
         compiler_params=pltpu.CompilerParams(vmem_limit_bytes=8 * 1024 * 1024),
         name="store",
-    )(ov, obs, trace)
+    )(ov, box, info, trace)
 
 
 def body(fields, rows, cols, rf, cf, w, order):
-    ov, obs, trace = run_main(fields, rows, cols, rf, cf, w, order)
-    adjoint, observed, trace = run_store(ov, obs, trace)
+    ov, box, info, trace = run_main(fields, rows, cols, rf, cf, w, order)
+    adjoint, observed, trace = run_store(ov, box, info, trace)
     return adjoint, observed, trace.reshape(())
 
 

time: 24.9 us -> 24.8 us (level)
  no operation moved by 1% of the time
where the time goes in v10:
time: 24.8 us; the launch traced here: 24.7 us
  Pallas kernels  24 us (97%)
  between operations  0.64 us (3%)
    pallas_call x1, Pallas kernels, run_main(): pl.pallas_call(main_kernel, out_shape=(pltpu.VMEM((64, 4, 8192), BF), plt...  21.4 us
    pallas_call x1, Pallas kernels, run_store(): pl.pallas_call(store_kernel, out_shape=(jax.ShapeDtypeStruct((64, 4, 8192...  2.64 us

profile of v10, /device:TPU:1, one launch (start us, length us, event | category | flops | bytes accessed | tf_op | source)
XLA Modules:
  0.0 24.7 jit_solution(8467064997488270681)
XLA Ops:
  0.6 21.4 %main.1 = (bf16[64,4,8192]{2,1,0:T(4,128)(2,1)S(1)}, f32[32,8,128]{2,1,0:T(8,128)S(1)}, f32[8,128]{1,0:T(8,128)S(1)}, f32[1,128]{1,0:T(1,128)S(1)}) custom-call(bf16[64,4,8192]{2,1,0:T(4,128)(2,1)} %x_ref.1, s32[32,128]{1,0:T(8,128)} %bitcast.8, s32[1,4096]{1,0:T(1,128)} %bitcast.9, s32[32,128]{1,0:T(8,128)} %bitcast.10, s32[32,128]{1,0:T(8,128)} %bitcast.11, ...), custom_call_target="tpu_custom_call" | custom-call | tf_op jit(solution)/shard_map/main/pallas_call | solution.py:382
  22.0 2.6 %store.1 = (bf16[64,4,8192]{2,1,0:T(4,128)(2,1)}, f32[64,128]{1,0:T(8,128)}, f32[1,1]{1,0:T(1,128)}) custom-call(bf16[64,4,8192]{2,1,0:T(4,128)(2,1)S(1)} %get-tuple-element.10.ov, f32[32,8,128]{2,1,0:T(8,128)S(1)} %get-tuple-element.11.box, f32[8,128]{1,0:T(8,128)S(1)} %get-tuple-element.12.info, f32[1,128]{1,0:T(1,128)S(1)} %get-tuple-element.13.trace_in), custom_call_target="tpu_custom_call" | custom-call | tf_op jit(solution)/shard_map/store/pallas_call | solution.py:422

commit v11 on v10

--- a/solution.py
+++ b/solution.py
@@ -280,8 +280,7 @@
         return (mm(high, reduce) + mm(low, reduce)).reshape(OWN, 8, 128)
 
     factor_b = prepare(1)
-    factor_a = []
-    mine_b[...] = forward(1, factor_b, lambda: factor_a.append(prepare(0)))
+    mine_b[...] = forward(1, factor_b, None)
     pl.semaphore_wait(barrier, OWN + 2)
     for d in range(1, 4):
         pl.semaphore_signal(
@@ -292,7 +291,8 @@
         {"slab": lax.rem(s + OWN - 1, OWN), "probe": z}, MESH,
     )
     to_prev.start()
-    mine_a[...] = forward(0, factor_a[0], None)
+    factor_a = prepare(0)
+    mine_a[...] = forward(0, factor_a, None)
     to_next = pltpu.make_async_remote_copy(
         mine_a, prev_box, halo_send.at[1], halo_recv.at[1],
         {"slab": lax.rem(s + 1, OWN), "probe": z}, MESH,

time: 24.8 us -> 25.1 us (1.012)
  Pallas kernels: 24 us -> 24.3 us
    pallas_call x1, Pallas kernels: 21.4 us -> 21.7 us  [run_main(): pl.pallas_call(main_kernel, out_shape=(pltpu.VMEM((64, 4, 8192), BF), plt...]
where the time goes in v11:
time: 25.1 us; the launch traced here: 24.9 us
  Pallas kernels  24.3 us (97%)
  between operations  0.64 us (3%)
    pallas_call x1, Pallas kernels, run_main(): pl.pallas_call(main_kernel, out_shape=(pltpu.VMEM((64, 4, 8192), BF), plt...  21.7 us
    pallas_call x1, Pallas kernels, run_store(): pl.pallas_call(store_kernel, out_shape=(jax.ShapeDtypeStruct((64, 4, 8192...  2.64 us

profile of v11, /device:TPU:1, one launch (start us, length us, event | category | flops | bytes accessed | tf_op | source)
XLA Modules:
  0.0 24.9 jit_solution(13914049477487563638)
XLA Ops:
  0.6 21.7 %main.1 = (bf16[64,4,8192]{2,1,0:T(4,128)(2,1)S(1)}, f32[32,8,128]{2,1,0:T(8,128)S(1)}, f32[8,128]{1,0:T(8,128)S(1)}, f32[1,128]{1,0:T(1,128)S(1)}) custom-call(bf16[64,4,8192]{2,1,0:T(4,128)(2,1)} %x_ref.1, s32[32,128]{1,0:T(8,128)} %bitcast.8, s32[1,4096]{1,0:T(1,128)} %bitcast.9, s32[32,128]{1,0:T(8,128)} %bitcast.10, s32[32,128]{1,0:T(8,128)} %bitcast.11, ...), custom_call_target="tpu_custom_call" | custom-call | tf_op jit(solution)/shard_map/main/pallas_call | solution.py:382
  22.3 2.6 %store.1 = (bf16[64,4,8192]{2,1,0:T(4,128)(2,1)}, f32[64,128]{1,0:T(8,128)}, f32[1,1]{1,0:T(1,128)}) custom-call(bf16[64,4,8192]{2,1,0:T(4,128)(2,1)S(1)} %get-tuple-element.10.ov, f32[32,8,128]{2,1,0:T(8,128)S(1)} %get-tuple-element.11.box, f32[8,128]{1,0:T(8,128)S(1)} %get-tuple-element.12.info, f32[1,128]{1,0:T(1,128)S(1)} %get-tuple-element.13.trace_in), custom_call_target="tpu_custom_call" | custom-call | tf_op jit(solution)/shard_map/store/pallas_call | solution.py:422
